TPU v7x, 8 devices: a whole 2x2x1 slice. The times are simulated.
8 devices in a mesh: fsdp: 2 (over z, y), tp: 4 (over x, core).
Axes of the slice: x: 2, y: 2, z: 1, core: 2. Of those that a mesh axis runs over, the one named last changes fastest.
Arguments:
- x: bfloat16 [16384, 6144], P(('fsdp', 'tp'))
- gamma: float32 [6144], replicated
- w1: bfloat16 [6144, 24576], P('fsdp', 'tp')
- w2: bfloat16 [24576, 6144], P('tp', 'fsdp')
Outputs:
- output: bfloat16 [16384, 6144], P(('fsdp', 'tp'))
All inputs are finite; a program needn't handle non-finite values.
Results may differ from a plain program's by a relative error of at most 0.001.
Values are sent between devices in bfloat16 or wider.
A program may use at most 1 GiB of HBM per device.

v0:
```python
import jax
import jax.numpy as jnp
from jax import lax
from jax.sharding import PartitionSpec as P

EPS = 1e-6


def _norm(x, gamma):
    xf = x.astype(jnp.float32)
    mu = jnp.mean(xf, axis=-1, keepdims=True)
    var = jnp.mean(jnp.square(xf - mu), axis=-1, keepdims=True)
    return xf, ((xf - mu) * lax.rsqrt(var + EPS) * gamma).astype(jnp.bfloat16)


def solution(mesh):
    def body(x, gamma, w1, w2):
        w1f = lax.all_gather(w1, "fsdp", axis=0, tiled=True)
        w2f = lax.all_gather(w2, "fsdp", axis=1, tiled=True)
        xf, xn = _norm(x, gamma)
        xg = lax.all_gather(xn, "tp", axis=0, tiled=True)
        h = jax.nn.gelu(jnp.dot(xg, w1f, preferred_element_type=jnp.float32), approximate=True).astype(jnp.bfloat16)
        yp = jnp.dot(h, w2f, preferred_element_type=jnp.float32)
        y = lax.psum_scatter(yp, "tp", scatter_dimension=0, tiled=True)
        return (xf + y).astype(jnp.bfloat16)

    return jax.shard_map(
        body,
        mesh=mesh,
        in_specs=(P(("fsdp", "tp"), None), P(None), P("fsdp", "tp"), P("tp", "fsdp")),
        out_specs=P(("fsdp", "tp"), None),
        check_vma=False,
    )
```

profile of v0, /device:TPU:0, one launch (start us, length us, event | category | flops | bytes accessed | tf_op | source)
XLA Modules:
  0.0 4332.4 jit_solution(4391445172051881073)
XLA Ops:
  6.5 0.0 copy-start
  6.5 0.0 all-gather.6.cloned.1.call-start
  6.5 0.7 all-gather.6.cloned.1.call-update
  7.3 0.0 all-gather.4.cloned.1.call-start
  7.3 9.8 convert_reduce_fusion
  17.1 11.4 fusion.16
  28.6 0.0 copy-done
  28.6 23.4 fusion.18
  52.0 0.0 all-gather.4.cloned.1.call-update
  52.1 0.0 all-gather.8.cloned.1.call-start
  52.1 0.7 all-gather.8.cloned.1.call-update
  52.8 0.0 reduce-scatter.2.cloned.1.call-start
  52.8 816.4 %all-gather.6.cloned.1.call-done = bf16[6144,6144]{1,0:T(8,128)(2,1)} async-done(((bf16[3072,6144]{1,0:T(8,128)(2,1)}), bf16[6144,6144]{1,0:T(8,128)(2,1)}) %all-gather.6.cloned.1.call-update) | async-done | bytes 75497488 | tf_op jit(solution)/shard_map/all_gather | solution.py:18
  869.3 581.6 %all-gather.4.cloned.1.call-done = bf16[8192,6144]{1,0:T(8,128)(2,1)} async-done(((bf16[2048,6144]{1,0:T(8,128)(2,1)}), bf16[8192,6144]{1,0:T(8,128)(2,1)}) %all-gather.4.cloned.1.call-update) | async-done | bytes 100663312 | tf_op jit(solution)/shard_map/all_gather | solution.py:21
  1450.8 642.3 %fusion.24 = f32[8192,6144]{1,0:T(8,128)} fusion(bf16[8192,6144]{1,0:T(8,128)(2,1)} %all-gather.4.cloned.1.call-done, bf16[6144,6144]{1,0:T(8,128)(2,1)} %all-gather.6.cloned.1.call-done), kind=kOutput, calls=%fused_computation.29 | convolution fusion | flops 618475290624 | bytes 377487360 | tf_op jit(solution)/shard_map/dot_general | solution.py:22
  2093.2 219.0 %all-gather.8.cloned.1.call-done = bf16[6144,6144]{1,0:T(8,128)(2,1)} async-done(((bf16[6144,3072]{1,0:T(8,128)(2,1)}), bf16[6144,6144]{1,0:T(8,128)(2,1)}) %all-gather.8.cloned.1.call-update) | async-done | bytes 75497488 | tf_op jit(solution)/shard_map/all_gather | solution.py:19
  2312.1 712.9 %fusion.8 = f32[8192,6144]{1,0:T(8,128)} fusion(bf16[6144,6144]{1,0:T(8,128)(2,1)} %all-gather.8.cloned.1.call-done, f32[8192,6144]{1,0:T(8,128)} %fusion.24), kind=kOutput, calls=%fused_computation.9 | convolution fusion | flops 618928275456 | bytes 478150656 | tf_op jit(solution)/shard_map/dot_general | solution.py:23
  3025.1 0.0 reduce-scatter.2.cloned.1.call-update
  3025.1 1268.4 %reduce-scatter.2.cloned.1.call-done = f32[2048,6144]{1,0:T(8,128)} async-done(((f32[8192,6144]{1,0:T(8,128)}), f32[2048,6144]{1,0:T(8,128)}) %reduce-scatter.2.cloned.1.call-update) | async-done | bytes 50331664 | tf_op jit(solution)/shard_map/reduce_scatter | solution.py:24
  4293.5 32.4 fusion.19
  (2 shorter events, 0.0 us)
Async XLA Ops:
  6.5 22.1 copy-start
  6.5 862.7 %all-gather.6.cloned.1.call-start = ((), (), s32[]{:S(2)}) async-start(), calls=%async_computation.2 | async-start | bytes 113246208 | tf_op jit(solution)/shard_map/all_gather | solution.py:18
  7.3 1443.6 %all-gather.4.cloned.1.call-start = ((), (), s32[]{:S(2)}) async-start(), calls=%async_computation.1 | async-start | bytes 125829120 | tf_op jit(solution)/shard_map/all_gather | solution.py:21
  52.1 2260.1 %all-gather.8.cloned.1.call-start = ((), (), s32[]{:S(2)}) async-start(), calls=%async_computation.3 | async-start | bytes 113246208 | tf_op jit(solution)/shard_map/all_gather | solution.py:19
  52.8 4240.7 %reduce-scatter.2.cloned.1.call-start = ((), (), s32[]{:S(2)}) async-start(), calls=%async_computation.4 | async-start | bytes 251658240 | tf_op jit(solution)/shard_map/reduce_scatter | solution.py:24
Sparse Core Ops, SparseCore 0:
  8.8 860.3 all-gather.5
  870.8 579.9 all-gather.3
  1452.4 859.7 all-gather.7
  3025.2 1268.2 reduce-scatter.1
where the time goes:
time: 4330 us
  waiting for transfers between devices  2890 us (67%)
  matrix products  1360 us (31%)
  other arithmetic  77.1 us (2%)
    reduce_scatter x1, waiting for transfers between devices, body(): y = lax.psum_scatter(yp, 'tp', scatter_dimension=0, tiled=True)  1270 us
    all_gather x1, waiting for transfers between devices, body(): w1f = lax.all_gather(w1, 'fsdp', axis=0, tiled=True)  816 us
    dot_general x1, matrix products, body(): yp = jnp.dot(h, w2f, preferred_element_type=jnp.float32)  713 us
    dot_general x1, matrix products, body(): jnp.dot(xg, w1f, preferred_element_type=jnp.float32)  642 us
    all_gather x1, waiting for transfers between devices, body(): xg = lax.all_gather(xn, 'tp', axis=0, tiled=True)  582 us
    all_gather x1, waiting for transfers between devices, body(): w2f = lax.all_gather(w2, 'fsdp', axis=1, tiled=True)  219 us
  transfers between devices with their start and end apart: 4, of which 4 were waited for; matrix products, arithmetic and copies ran while one was open for 16% of the time, Pallas kernels for 0%

commit v1 on v0

v1 whole, which is shorter than its diff:
```python
import functools

import jax
import jax.numpy as jnp
from jax import lax
from jax.experimental import pallas as pl
from jax.experimental.pallas import tpu as pltpu
from jax.sharding import PartitionSpec as P

EPS = 1e-6
F32 = jnp.float32
BF16 = jnp.bfloat16
MESH = pl.DeviceIdType.MESH

N1 = 12
N2 = 6
NX = 8
AHEAD = 3
LAG = 2


def _where(cond, a, b):
    return jnp.where(cond, jnp.int32(a), jnp.int32(b))


def _mm1_step(s):
    segs = (
        (0, 0, 2, 0),
        (16, 0, 1, 2),
        (24, 4, 3, 0),
        (48, 0, 1, 3),
        (64, 8, 2, 2),
        (76, 8, 2, 0),
        (80, 11, 2, 2),
        (84, 9, 2, 0),
    )
    start, c0, nm, m0 = (jnp.int32(v) for v in segs[0])
    for g in segs[1:]:
        late = s >= g[0]
        start, c0, nm, m0 = (_where(late, new, old) for new, old in zip(g, (start, c0, nm, m0)))
    u = s - start
    pair = u // nm
    return c0 + pair // 2, pair % 2, m0 + u % nm


def _mm2_visit(v):
    n = 2 * N2
    u = v - LAG
    mid_own = u % 2
    mid = _where(mid_own == 1, u // 2, LAG + u // 2)
    own = _where(v < LAG, 0, _where(v < 2 * n - LAG, mid_own, 1))
    k = _where(v < LAG, v, _where(v < 2 * n - LAG, mid, v - n))
    return own, k


def _kernel(
    x, gamma, w1, w2,
    y, xn, w1far, w1so, w1sf, w2far, w2so, w2sf, h, psend, precv,
    act, wb, hout, pout, pin, xin, yout, gam,
    act_sem, w_sem, h_sem, io_sem,
    xn_s, xn_r, w1y_s, w1y_r, w1c_s, w1c_r, w1f_s, w1f_r,
    w2y_s, w2y_r, w2c_s, w2c_r, w2f_s, w2f_r, p_s, p_r,
):
    a = lax.axis_index("fsdp")
    b = lax.axis_index("tp")
    to_y = {"fsdp": 1 - a}
    to_x = {"tp": lax.rem(b + 2, 4)}
    to_c = {"tp": b + 1 - 2 * lax.rem(b, 2)}
    rows, d = x.shape
    half, fq = w1.shape
    sub = rows // 4
    tile = rows // 2
    c1 = fq // N1
    c2 = half // N2
    piece = rows // NX
    near = pl.multiple_of(a * half, half)
    away = pl.multiple_of((1 - a) * half, half)

    def remote(src, dst, ssem, rsem, to):
        return pltpu.make_async_remote_copy(
            src_ref=src, dst_ref=dst, send_sem=ssem, recv_sem=rsem, device_id=to, device_id_type=MESH
        )

    def cols1(j):
        return pl.ds(pl.multiple_of(j * c1, c1), c1)

    def cols2(k):
        return pl.ds(pl.multiple_of(k * c2, c2), c2)

    def w1_y(j):
        return remote(w1.at[:, cols1(j)], w1far.at[:, cols1(j)], w1y_s.at[j], w1y_r.at[j], to_y)

    def w1_c(j):
        return remote(w1.at[:, cols1(j)], w1so.at[:, cols1(j)], w1c_s.at[j], w1c_r.at[j], to_c)

    def w1_f(j):
        return remote(w1far.at[:, cols1(j)], w1sf.at[:, cols1(j)], w1f_s.at[j], w1f_r.at[j], to_c)

    def w2_y(k):
        return remote(w2.at[:, cols2(k)], w2far.at[:, cols2(k)], w2y_s.at[k], w2y_r.at[k], to_y)

    def w2_c(k):
        return remote(w2.at[:, cols2(k)], w2so.at[:, cols2(k)], w2c_s.at[k], w2c_r.at[k], to_c)

    def w2_f(k):
        return remote(w2far.at[:, cols2(k)], w2sf.at[:, cols2(k)], w2f_s.at[k], w2f_r.at[k], to_c)

    def xrows(t):
        return pl.ds(pl.multiple_of(t * piece, piece), piece)

    def xn_x(t):
        return remote(xn.at[xrows(t)], xn.at[xrows(t + NX)], xn_s.at[t], xn_r.at[t], to_x)

    def p_x(i, k):
        at = (pl.ds(pl.multiple_of(i * sub, sub), sub), cols2(k))
        return remote(psend.at[at], precv.at[at], p_s.at[k * 4 + i], p_r.at[k * 4 + i], to_x)

    barrier = pltpu.get_barrier_semaphore()
    for to in (to_y, to_x, to_c):
        pl.semaphore_signal(barrier, inc=1, device_id=to, device_id_type=MESH)
    pl.semaphore_wait(barrier, 3)

    for j in range(AHEAD):
        w1_y(j).start()

    @pl.loop(0, N1)
    def _(j):
        w1_c(j).start()

    for i, off in enumerate((near, away)):
        g = pltpu.make_async_copy(gamma.at[:, pl.ds(off, half)], gam.at[:, i * half : (i + 1) * half], io_sem.at[i])
        g.start()

    def x_in(t, slot):
        return [
            pltpu.make_async_copy(
                x.at[xrows(t), pl.ds(off, half)],
                act.at[slot, 0:piece, i * half : (i + 1) * half],
                act_sem.at[slot, i],
            )
            for i, off in enumerate((near, away))
        ]

    for c in x_in(0, 0):
        c.start()
    for i, off in enumerate((near, away)):
        pltpu.make_async_copy(
            gamma.at[:, pl.ds(off, half)], gam.at[:, i * half : (i + 1) * half], io_sem.at[i]
        ).wait()

    @pl.loop(0, NX)
    def _(t):
        slot = t % 2

        @pl.when(t + 1 < NX)
        def _():
            for c in x_in(t + 1, 1 - slot):
                c.start()

        for c in x_in(t, slot):
            c.wait()

        @pl.loop(0, piece // 16)
        def _(r):
            at = pl.multiple_of(r * 16, 16)
            xs = act[slot, pl.ds(at, 16), 0:d].astype(F32)
            xc = xs - jnp.mean(xs, axis=1, keepdims=True)
            var = jnp.mean(xc * xc, axis=1, keepdims=True)
            act[slot, pl.ds(piece + at, 16), 0:d] = (xc * lax.rsqrt(var + EPS) * gam[...]).astype(BF16)

        out = pltpu.make_async_copy(act.at[slot, piece : 2 * piece, 0:d], xn.at[xrows(t)], io_sem.at[2])
        out.start()
        out.wait()

        @pl.when(t < NX // 2)
        def _():
            xn_x(t).start()

    def a1_in(m, slot):
        return [
            pltpu.make_async_copy(
                xn.at[pl.ds(pl.multiple_of(m * tile + r * sub, sub), sub)],
                act.at[slot, :, r * d : (r + 1) * d],
                act_sem.at[slot, r],
            )
            for r in range(2)
        ]

    def w1_in(j, q, slot, go):
        def pair(own, far):
            for i, ref in enumerate((own, far)):
                c = pltpu.make_async_copy(
                    ref.at[:, cols1(j)], wb.at[slot, i * half : (i + 1) * half], w_sem.at[slot, i]
                )
                c.start() if go else c.wait()

        if not go:
            pair(w1, w1far)
            return

        @pl.when(q == 0)
        def _():
            pair(w1, w1far)

        @pl.when(q == 1)
        def _():
            pair(w1so, w1sf)

    def arrive1(s):
        j, q, m = _mm1_step(s)
        first = m == _where(j < 8, 0, 2)

        @pl.when(first & (q == 0))
        def _():
            w1_y(j).wait_recv()
            w1_f(j).start()

            @pl.when(j + AHEAD < N1)
            def _():
                w1_y(j + AHEAD).start()

            @pl.when(j + AHEAD >= N1)
            def _():
                w2_y(j + AHEAD - N1).start()

            @pl.when(j == 2)
            def _():
                for t in range(NX // 2, NX):
                    xn_x(t).start()

            @pl.when(j == 4)
            def _():
                for k in range(N2):
                    w2_c(k).start()

        @pl.when(first & (q == 1))
        def _():
            w1_c(j).wait_recv()
            w1_f(j).wait_recv()

        @pl.when(s == 16)
        def _():
            for t in range(NX // 2):
                xn_x(t).wait_recv()

        @pl.when(s == 48)
        def _():
            for t in range(NX // 2, NX):
                xn_x(t).wait_recv()

    def load1(s, aslot, wslot, a_new, w_new):
        j, q, m = _mm1_step(s)

        @pl.when(a_new)
        def _():
            for c in a1_in(m, aslot):
                c.start()

        @pl.when(w_new)
        def _():
            w1_in(j, q, wslot, True)

    def h_out(s):
        j, q, m = _mm1_step(s)
        col = pl.multiple_of(q * fq + j * c1, c1)
        return pltpu.make_async_copy(
            hout.at[s % 2], h.at[pl.ds(pl.multiple_of(m * tile, tile), tile), pl.ds(col, c1)], h_sem.at[s % 2]
        )

    def first_product(lo, hi):
        arrive1(lo)
        load1(lo, 0, 0, True, True)

        def step(s, carry):
            aslot, wslot, a_fresh, w_fresh = carry
            j, q, m = _mm1_step(s)
            nj, nq, nm = _mm1_step(s + 1)
            more = s + 1 < hi
            a_new = more & (nm != m)
            w_new = more & ((nj != j) | (nq != q))
            na = _where(a_new, 1 - aslot, aslot)
            nw = _where(w_new, 1 - wslot, wslot)

            @pl.when(more)
            def _():
                arrive1(s + 1)

            load1(s + 1, na, nw, a_new, w_new)

            @pl.when(a_fresh == 1)
            def _():
                for c in a1_in(m, aslot):
                    c.wait()

            @pl.when(w_fresh == 1)
            def _():
                w1_in(j, q, wslot, False)

            @pl.when(s >= lo + 2)
            def _():
                h_out(s - 2).wait()

            for r in range(2):
                u = jnp.dot(act[aslot, :, r * d : (r + 1) * d], wb[wslot, 0:d], preferred_element_type=F32)
                hout[s % 2, r * sub : (r + 1) * sub] = jax.nn.gelu(u, approximate=True).astype(BF16)
            h_out(s).start()
            return na, nw, _where(a_new, 1, 0), _where(w_new, 1, 0)

        one, nil = jnp.int32(1), jnp.int32(0)
        lax.fori_loop(lo, hi, step, (nil, nil, one, one))
        h_out(hi - 2).wait()
        h_out(hi - 1).wait()

    def a2_in(own, i, slot):
        at = pl.multiple_of(_where(own == 1, 0, rows) + i * sub, sub)
        return pltpu.make_async_copy(h.at[pl.ds(at, sub)], act.at[slot], act_sem.at[slot, 0])

    def w2_in(k, slot, go):
        def pair(kk, own, sib):
            for i, ref in enumerate((own, sib)):
                c = pltpu.make_async_copy(
                    ref.at[:, cols2(kk)], wb.at[slot, i * fq : (i + 1) * fq], w_sem.at[slot, i]
                )
                c.start() if go else c.wait()

        if not go:
            pair(0, w2, w2so)
            return

        @pl.when(k < N2)
        def _():
            pair(k, w2, w2so)

        @pl.when(k >= N2)
        def _():
            pair(k - N2, w2far, w2sf)

    def arrive2(v):
        own, k = _mm2_visit(v)

        @pl.when((own == 0) & (k < N2))
        def _():
            w2_c(k).wait_recv()

        @pl.when((own == 0) & (k >= N2))
        def _():
            w2_f(k - N2).wait_recv()

        @pl.when((own == 0) & (k >= 1) & (k + AHEAD - 1 < N2))
        def _():
            w2_y(k + AHEAD - 1).start()

        @pl.when((own == 1) & (k >= 3) & (k < 3 + N2))
        def _():
            w2_y(k - 3).wait_recv()
            w2_f(k - 3).start()

    def second_product(lo, hi):
        arrive2(lo)
        own0, k0 = _mm2_visit(lo)
        a2_in(own0, 0, 0).start()
        w2_in(k0, 0, True)

        def step(s, carry):
            v, i = s // 4, s % 4
            own, k = _mm2_visit(v)
            aslot = (s - lo * 4) % 2
            wslot = (v - lo) % 2
            more = s + 1 < hi * 4
            nv, ni = (s + 1) // 4, (s + 1) % 4
            nown, nk = _mm2_visit(nv)

            @pl.when(more & (ni == 0))
            def _():
                arrive2(nv)
                w2_in(nk, 1 - wslot, True)

            @pl.when(more)
            def _():
                a2_in(nown, ni, 1 - aslot).start()

            a2_in(own, i, aslot).wait()

            @pl.when(i == 0)
            def _():
                w2_in(k, wslot, False)

            at = pl.ds(pl.multiple_of(i * sub, sub), sub)
            ycol = pl.multiple_of(_where(k < N2, near, away) + (k % N2) * c2, c2)
            x_tile = pltpu.make_async_copy(x.at[at, pl.ds(ycol, c2)], xin, io_sem.at[0])
            y_tile = pltpu.make_async_copy(yout, y.at[at, pl.ds(ycol, c2)], io_sem.at[3])

            @pl.when(own == 1)
            def _():
                x_tile.start()

            pout[...] = jnp.dot(act[aslot], wb[wslot], preferred_element_type=F32)

            @pl.when(own == 0)
            def _():
                out = pltpu.make_async_copy(pout, psend.at[at, cols2(k)], io_sem.at[1])
                out.start()
                out.wait()
                p_x(i, k).start()

            @pl.when(own == 1)
            def _():
                p_x(i, k).wait_recv()
                got = pltpu.make_async_copy(precv.at[at, cols2(k)], pin, io_sem.at[2])
                got.start()
                x_tile.wait()
                got.wait()
                yout[...] = (xin[...].astype(F32) + (pout[...] + pin[...])).astype(BF16)
                y_tile.start()
                y_tile.wait()

            return carry

        lax.fori_loop(lo * 4, hi * 4, step, jnp.int32(0))

    @pl.loop(0, 2)
    def _(phase):
        first_product(_where(phase == 0, 0, 84), _where(phase == 0, 84, 96))
        second_product(_where(phase == 0, 0, LAG), _where(phase == 0, LAG, 4 * N2))

    @pl.loop(0, N1)
    def _(j):
        w1_y(j).wait_send()
        w1_c(j).wait_send()
        w1_f(j).wait_send()

    @pl.loop(0, N2)
    def _(k):
        w2_y(k).wait_send()
        w2_c(k).wait_send()
        w2_f(k).wait_send()

    @pl.loop(0, NX)
    def _(t):
        xn_x(t).wait_send()

    @pl.loop(0, 2 * N2 * 4)
    def _(s):
        p_x(s % 4, s // 4).wait_send()


def solution(mesh):
    def body(x, gamma, w1, w2):
        rows, d = x.shape
        half, fq = w1.shape
        sub = rows // 4
        c1, c2 = fq // N1, half // N2

        def hbm(shape, dtype):
            return jax.ShapeDtypeStruct(shape, dtype)

        dma = pltpu.SemaphoreType.DMA
        outs = pl.pallas_call(
            _kernel,
            name="mlp",
            out_shape=(
                hbm((rows, d), BF16),
                hbm((2 * rows, d), BF16),
                hbm((half, fq), BF16),
                hbm((half, fq), BF16),
                hbm((half, fq), BF16),
                hbm((fq, half), BF16),
                hbm((fq, half), BF16),
                hbm((fq, half), BF16),
                hbm((2 * rows, 2 * fq), BF16),
                hbm((rows, d), F32),
                hbm((rows, d), F32),
            ),
            in_specs=[pl.BlockSpec(memory_space=pl.ANY)] * 4,
            out_specs=tuple([pl.BlockSpec(memory_space=pl.ANY)] * 11),
            scratch_shapes=[
                pltpu.VMEM((2, sub, 2 * d), BF16),
                pltpu.VMEM((2, 2 * fq, c2), BF16),
                pltpu.VMEM((2, 2 * sub, c1), BF16),
                pltpu.VMEM((sub, c2), F32),
                pltpu.VMEM((sub, c2), F32),
                pltpu.VMEM((sub, c2), BF16),
                pltpu.VMEM((sub, c2), BF16),
                pltpu.VMEM((1, d), F32),
                dma((2, 2)), dma((2, 2)), dma((2,)), dma((4,)),
                dma((NX,)), dma((NX,)),
                dma((N1,)), dma((N1,)), dma((N1,)), dma((N1,)), dma((N1,)), dma((N1,)),
                dma((N2,)), dma((N2,)), dma((N2,)), dma((N2,)), dma((N2,)), dma((N2,)),
                dma((8 * N2,)), dma((8 * N2,)),
            ],
            compiler_params=pltpu.CompilerParams(
                collective_id=0, has_side_effects=True, vmem_limit_bytes=66_000_000
            ),
        )(x, gamma.reshape(1, d), w1, w2)
        return outs[0]

    return jax.shard_map(
        body,
        mesh=mesh,
        in_specs=(P(("fsdp", "tp"), None), P(None), P("fsdp", "tp"), P("tp", "fsdp")),
        out_specs=P(("fsdp", "tp"), None),
        check_vma=False,
    )
```

time: 4330 us -> 1980 us (0.46)
  waiting for transfers between devices: 2890 us -> 0 us
  Pallas kernels: 0 us -> 1950 us
  matrix products: 1360 us -> 0 us
  other arithmetic: 77.1 us -> 0 us
    pallas_call x0 -> x1, Pallas kernels: none -> 1950 us  [body(): pl.pallas_call(_kernel, name='mlp', out_shape=(hbm((rows, d), BF16), hbm(...]
    all_gather x3 -> x0, waiting for transfers between devices: 1620 us -> none  [the longest x1 816 us: body(): w1f = lax.all_gather(w1, 'fsdp', axis=0, tiled=True)]
    dot_general x2 -> x0, matrix products: 1360 us -> none  [the longest x1 713 us: body(): yp = jnp.dot(h, w2f, preferred_element_type=jnp.float32)]
    reduce_scatter x1 -> x0, waiting for transfers between devices: 1270 us -> none  [body(): y = lax.psum_scatter(yp, 'tp', scatter_dimension=0, tiled=True)]
    convert_element_type x2 -> x0, other arithmetic: 55.8 us -> none  [the longest x1 32.4 us: body(): return (xf + y).astype(jnp.bfloat16)]
  transfers between devices with their start and end apart: 4 -> 0, of which waited for: 4 -> 0; matrix products, arithmetic and copies ran while one was open for 16% -> 0% of each run, Pallas kernels for 0% -> 0%
where the time goes in v1:
time: 1980 us
  Pallas kernels  1950 us (98%)
  local copies, waits for them, and re-layouts  21 us (1%)
    pallas_call x1, Pallas kernels, body(): pl.pallas_call(_kernel, name='mlp', out_shape=(hbm((rows, d), BF16), hbm(...  1950 us

profile of v1, /device:TPU:0, one launch (start us, length us, event | category | flops | bytes accessed | tf_op | source)
XLA Modules:
  0.0 1975.1 jit_solution(8097653417896397885)
XLA Ops:
  0.0 1954.1 %mlp.1 = (bf16[2048,6144]{1,0:T(8,128)(2,1)}, bf16[4096,6144]{1,0:T(8,128)(2,1)}, bf16[3072,6144]{1,0:T(8,128)(2,1)}, bf16[3072,6144]{1,0:T(8,128)(2,1)}, bf16[3...) custom-call(bf16[2048,6144]{1,0:T(8,128)(2,1)} %x.1, ...), custom_call_target="tpu_custom_call" | custom-call | tf_op jit(solution)/shard_map/mlp/pallas_call | solution.py:458
  1954.1 21.0 %copy.6 = bf16[2048,6144]{1,0:T(8,128)(2,1)} copy(bf16[2048,6144]{1,0:T(8,128)(2,1)} %get-tuple-element.6) | data formatting | bytes 50331648

commit v2 on v1

--- a/solution.py
+++ b/solution.py
@@ -16,7 +16,7 @@
 N2 = 6
 NX = 8
 AHEAD = 3
-LAG = 2
+LAG = 3
 
 
 def _where(cond, a, b):
@@ -31,8 +31,6 @@
         (48, 0, 1, 3),
         (64, 8, 2, 2),
         (76, 8, 2, 0),
-        (80, 11, 2, 2),
-        (84, 9, 2, 0),
     )
     start, c0, nm, m0 = (jnp.int32(v) for v in segs[0])
     for g in segs[1:]:
@@ -57,7 +55,7 @@
     x, gamma, w1, w2,
     y, xn, w1far, w1so, w1sf, w2far, w2so, w2sf, h, psend, precv,
     act, wb, hout, pout, pin, xin, yout, gam,
-    act_sem, w_sem, h_sem, io_sem,
+    act_sem, w_sem, h_sem, io_sem, tail_sem,
     xn_s, xn_r, w1y_s, w1y_r, w1c_s, w1c_r, w1f_s, w1f_r,
     w2y_s, w2y_r, w2c_s, w2c_r, w2f_s, w2f_r, p_s, p_r,
 ):
@@ -72,6 +70,8 @@
     tile = rows // 2
     c1 = fq // N1
     c2 = half // N2
+    cb = c1 // 2
+    t0 = fq - c1
     piece = rows // NX
     near = pl.multiple_of(a * half, half)
     away = pl.multiple_of((1 - a) * half, half)
@@ -95,6 +95,17 @@
 
     def w1_f(j):
         return remote(w1far.at[:, cols1(j)], w1sf.at[:, cols1(j)], w1f_s.at[j], w1f_r.at[j], to_c)
+
+    def cols_t(t):
+        return pl.ds(t0 + t * cb, cb)
+
+    def w1_yt(t):
+        at = (slice(None), cols_t(t))
+        return remote(w1.at[at], w1far.at[at], w1y_s.at[N1 - 1 + t], w1y_r.at[N1 - 1 + t], to_y)
+
+    def w1_ft(t):
+        at = (slice(None), cols_t(t))
+        return remote(w1far.at[at], w1sf.at[at], w1f_s.at[N1 - 1 + t], w1f_r.at[N1 - 1 + t], to_c)
 
     def w2_y(k):
         return remote(w2.at[:, cols2(k)], w2far.at[:, cols2(k)], w2y_s.at[k], w2y_r.at[k], to_y)
@@ -215,13 +226,14 @@
             w1_y(j).wait_recv()
             w1_f(j).start()
 
-            @pl.when(j + AHEAD < N1)
+            @pl.when(j + AHEAD < N1 - 1)
             def _():
                 w1_y(j + AHEAD).start()
 
-            @pl.when(j + AHEAD >= N1)
-            def _():
-                w2_y(j + AHEAD - N1).start()
+            @pl.when(j + AHEAD == N1 - 1)
+            def _():
+                w1_yt(0).start()
+                w1_yt(1).start()
 
             @pl.when(j == 2)
             def _():
@@ -350,10 +362,10 @@
         def _():
             w2_y(k + AHEAD - 1).start()
 
-        @pl.when((own == 1) & (k >= 3) & (k < 3 + N2))
-        def _():
-            w2_y(k - 3).wait_recv()
-            w2_f(k - 3).start()
+        @pl.when((own == 1) & (k >= 5 - LAG) & (k < 5 - LAG + N2))
+        def _():
+            w2_y(k - (5 - LAG)).wait_recv()
+            w2_f(k - (5 - LAG)).start()
 
     def second_product(lo, hi):
         arrive2(lo)
@@ -418,16 +430,134 @@
 
         lax.fori_loop(lo * 4, hi * 4, step, jnp.int32(0))
 
+    def junction():
+        def w_tail(t, part):
+            refs = ((w1, w1so), (w1far, w1sf))[part]
+            return [
+                pltpu.make_async_copy(
+                    refs[q].at[:, cols_t(t)],
+                    wb.at[0, t * d + part * half : t * d + (part + 1) * half, q * cb : (q + 1) * cb],
+                    tail_sem.at[t, part, q],
+                )
+                for q in range(2)
+            ]
+
+        def xn_in(i):
+            at = pl.multiple_of(rows + i * sub, sub)
+            return pltpu.make_async_copy(xn.at[pl.ds(at, sub)], act.at[1, :, 0:d], act_sem.at[1, 0])
+
+        def h_at(i, q, col, width):
+            return h.at[pl.ds(pl.multiple_of(rows + i * sub, sub), sub), q * fq + col : q * fq + col + width]
+
+        def h_in(i):
+            return [
+                pltpu.make_async_copy(h_at(i, q, 0, t0), act.at[0, :, q * fq : q * fq + t0], act_sem.at[0, q])
+                for q in range(2)
+            ]
+
+        def arrive(t):
+            w1_yt(t).wait_recv()
+            w1_ft(t).start()
+            if t == 1:
+                for k in range(AHEAD):
+                    w2_y(k).start()
+            w1_ft(t).wait_recv()
+            for c in w_tail(t, 1):
+                c.start()
+            for part in range(2):
+                for c in w_tail(t, part):
+                    c.wait()
+
+        w1_c(N1 - 1).wait_recv()
+        for t in range(2):
+            for c in w_tail(t, 0):
+                c.start()
+        xn_in(0).start()
+        for c in h_in(0):
+            c.start()
+        w2_c(0).wait_recv()
+        w2_in(jnp.int32(0), 1, True)
+        arrive(0)
+        w2_in(jnp.int32(0), 1, False)
+
+        def tile_(i, carry):
+            xn_in(i).wait()
+            u = jnp.dot(act[1, :, 0:d], wb[0, 0:d], preferred_element_type=F32)
+            g = jax.nn.gelu(u, approximate=True).astype(BF16)
+            for c in h_in(i):
+                c.wait()
+            first = []
+            for q in range(2):
+                act[0, :, q * fq + t0 : q * fq + t0 + cb] = g[:, q * cb : (q + 1) * cb]
+                first.append(
+                    pltpu.make_async_copy(
+                        act.at[0, :, q * fq + t0 : q * fq + t0 + cb], h_at(i, q, t0, cb), h_sem.at[q]
+                    )
+                )
+                first[-1].start()
+            n = fq - cb
+            pout[...] = jnp.dot(act[0, :, 0:n], wb[1, 0:n], preferred_element_type=F32) + jnp.dot(
+                act[0, :, fq : fq + n], wb[1, fq : fq + n], preferred_element_type=F32
+            )
+            for c in first:
+                c.wait()
+
+            @pl.when(i < 3)
+            def _():
+                for c in h_in(i + 1):
+                    c.start()
+
+            @pl.when(i == 0)
+            def _():
+                arrive(1)
+
+            u = jnp.dot(act[1, :, 0:d], wb[0, d : 2 * d], preferred_element_type=F32)
+            hout[0, 0:sub] = jax.nn.gelu(u, approximate=True).astype(BF16)
+
+            @pl.when(i < 3)
+            def _():
+                xn_in(i + 1).start()
+
+            second = []
+            for q in range(2):
+                second.append(
+                    pltpu.make_async_copy(
+                        hout.at[0, 0:sub, q * cb : (q + 1) * cb], h_at(i, q, t0 + cb, cb), h_sem.at[q]
+                    )
+                )
+                second[-1].start()
+            pout[...] += jnp.dot(hout[0, 0:sub, 0:cb], wb[1, n:fq], preferred_element_type=F32) + jnp.dot(
+                hout[0, 0:sub, cb : 2 * cb], wb[1, fq + n : 2 * fq], preferred_element_type=F32
+            )
+            at = pl.ds(pl.multiple_of(i * sub, sub), sub)
+            out = pltpu.make_async_copy(pout, psend.at[at, 0:c2], io_sem.at[1])
+            out.start()
+            out.wait()
+            p_x(i, 0).start()
+            for c in second:
+                c.wait()
+            return carry
+
+        lax.fori_loop(0, 4, tile_, jnp.int32(0))
+
     @pl.loop(0, 2)
     def _(phase):
-        first_product(_where(phase == 0, 0, 84), _where(phase == 0, 84, 96))
-        second_product(_where(phase == 0, 0, LAG), _where(phase == 0, LAG, 4 * N2))
+        first_product(_where(phase == 0, 0, 76), _where(phase == 0, 76, 92))
+        pl.when(phase == 0)(junction)
+        second_product(_where(phase == 0, 1, LAG), _where(phase == 0, LAG, 4 * N2))
+
+    @pl.loop(0, N1 - 1)
+    def _(j):
+        w1_y(j).wait_send()
+        w1_f(j).wait_send()
+
+    for t in range(2):
+        w1_yt(t).wait_send()
+        w1_ft(t).wait_send()
 
     @pl.loop(0, N1)
     def _(j):
-        w1_y(j).wait_send()
         w1_c(j).wait_send()
-        w1_f(j).wait_send()
 
     @pl.loop(0, N2)
     def _(k):
@@ -442,6 +572,10 @@
     @pl.loop(0, 2 * N2 * 4)
     def _(s):
         p_x(s % 4, s // 4).wait_send()
+
+
+def _put(src, dst):
+    dst[...] = src[...]
 
 
 def solution(mesh):
@@ -482,9 +616,9 @@
                 pltpu.VMEM((sub, c2), BF16),
                 pltpu.VMEM((sub, c2), BF16),
                 pltpu.VMEM((1, d), F32),
-                dma((2, 2)), dma((2, 2)), dma((2,)), dma((4,)),
+                dma((2, 2)), dma((2, 2)), dma((2,)), dma((4,)), dma((2, 2, 2)),
                 dma((NX,)), dma((NX,)),
-                dma((N1,)), dma((N1,)), dma((N1,)), dma((N1,)), dma((N1,)), dma((N1,)),
+                dma((N1 + 1,)), dma((N1 + 1,)), dma((N1,)), dma((N1,)), dma((N1 + 1,)), dma((N1 + 1,)),
                 dma((N2,)), dma((N2,)), dma((N2,)), dma((N2,)), dma((N2,)), dma((N2,)),
                 dma((8 * N2,)), dma((8 * N2,)),
             ],
@@ -492,7 +626,15 @@
                 collective_id=0, has_side_effects=True, vmem_limit_bytes=66_000_000
             ),
         )(x, gamma.reshape(1, d), w1, w2)
-        return outs[0]
+        block = pl.BlockSpec((rows // 8, d), lambda i: (i, 0))
+        return pl.pallas_call(
+            _put,
+            name="put",
+            out_shape=hbm((rows, d), BF16),
+            grid=(8,),
+            in_specs=[block],
+            out_specs=block,
+        )(outs[0])
 
     return jax.shard_map(
         body,

time: 1980 us -> 1930 us (0.975)
  local copies, waits for them, and re-layouts: 21 us -> 0 us
  Pallas kernels: 1950 us -> 1930 us
    pallas_call x1, Pallas kernels: 1950 us -> 1910 us  [body(): pl.pallas_call(_kernel, name='mlp', out_shape=(hbm((rows, d), BF16), hbm(...]
    unnamed x1 -> x0, local copies, waits for them, and re-layouts: 21 us -> none
where the time goes in v2:
time: 1930 us
  Pallas kernels  1930 us (100%)
    pallas_call x1, Pallas kernels, body(): pl.pallas_call(_kernel, name='mlp', out_shape=(hbm((rows, d), BF16), hbm(...  1910 us

profile of v2, /device:TPU:0, one launch (start us, length us, event | category | flops | bytes accessed | tf_op | source)
XLA Modules:
  0.0 1933.2 jit_solution(3607144162457370851)
XLA Ops:
  0.0 1914.9 %mlp.1 = (bf16[2048,6144]{1,0:T(8,128)(2,1)}, bf16[4096,6144]{1,0:T(8,128)(2,1)}, bf16[3072,6144]{1,0:T(8,128)(2,1)}, bf16[3072,6144]{1,0:T(8,128)(2,1)}, bf16[3...) custom-call(bf16[2048,6144]{1,0:T(8,128)(2,1)} %x.1, ...), custom_call_target="tpu_custom_call" | custom-call | tf_op jit(solution)/shard_map/mlp/pallas_call | solution.py:592
  1914.9 18.3 put.1

commit v3 on v0

v3 whole, which is shorter than its diff:
```python
import jax
import jax.numpy as jnp
from jax import lax
from jax.experimental import pallas as pl
from jax.experimental.pallas import tpu as pltpu
from jax.sharding import PartitionSpec as P

EPS = 1e-6
F32 = jnp.float32
BF16 = jnp.bfloat16
MESH = pl.DeviceIdType.MESH

N1 = 12
NR = N1 - 1
N2 = 6
NX = 8
AHEAD = 3

STEPS1 = (
    ((0, 4), (0, 2)),
    ((0, 4), (2, 1)),
    ((4, 2), (0, 3)),
    ((0, 3), (3, 1)),
    ((6, 1), (0, 3)),
    ((3, 4), (3, 1)),
    ((7, 1), (2, 2)),
    ((0, 8), (4, 1)),
    ((7, 1), (0, 2)),
    ((8, 2), (2, 3)),
    ((8, 5), (0, 2)),
)
BREAK1 = 10

REM, OWN, END = 0, 1, 2
R, A, B = ((lambda k, t=t: (t, k)) for t in (REM, OWN, END))
VISITS = (
    R(1), R(2), R(3), R(4),
    R(5), A(0), A(1), R(6), A(2), B(0), B(1), A(3), R(7), B(2), A(4), A(5), R(8), B(3), A(6), A(7), B(4), B(5),
    R(9), A(8), B(6), A(9), B(7), R(10), B(8), A(10), R(11), A(11), B(9), B(10), B(11),
)
BREAK2 = 4
PASS_F = {A(1): 0, B(1): 1, A(5): 2, B(5): 3, B(7): 4, R(11): 5}
PASS_G = {B(4): 0, A(11): 1}
SEND_F = {R(2): (2,), R(5): (3, 4), R(7): (5,)}
SEND_G = {R(2): 0, R(7): 1}


def _where(cond, a, b):
    return jnp.where(cond, jnp.int32(a), jnp.int32(b))


def _bounds1():
    at, out = 0, []
    for (_, nj), (_, nt) in STEPS1:
        out.append(at)
        at += nj * 2 * nt
    return out, at


def _step1(s):
    starts, _ = _bounds1()
    rows = [(at, j0, nt, t0) for at, ((j0, _), (t0, nt)) in zip(starts, STEPS1)]
    start, j0, nt, t0 = (jnp.int32(v) for v in rows[0])
    for row in rows[1:]:
        late = s >= row[0]
        start, j0, nt, t0 = (_where(late, new, old) for new, old in zip(row, (start, j0, nt, t0)))
    u = s - start
    pair = u // nt
    return j0 + pair // 2, pair % 2, t0 + u % nt


def _first_tile(j):
    return _where(j < 7, 0, _where(j < NR - 1, 2, _where(j == NR - 1, 9, 0)))


def _visit(v):
    code = jnp.int32(0)
    for n, (t, k) in enumerate(VISITS):
        code = _where(v == n, t * 16 + k, code)
    return code // 16, code % 16


def _kernel(
    x, gamma, w1, w2,
    y, xn, w1e, w1far, w1so, w1sf, w2e, w2far, w2so, w2sf, h, psend, pown, precv,
    act, wb, hout, pout, pin, pback, xin, yout, gam,
    act_sem, w_sem, h_sem, io_sem, out_sem, in_sem, tail_sem,
    xn_s, xn_r, e_s, e_r, w1y_s, w1y_r, w1c_s, w1c_r, w1f_s, w1f_r,
    w2y_s, w2y_r, w2c_s, w2c_r, w2f_s, w2f_r, p_s, p_r,
):
    a = lax.axis_index("fsdp")
    b = lax.axis_index("tp")
    to_y = {"fsdp": 1 - a}
    to_x = {"tp": lax.rem(b + 2, 4)}
    to_c = {"tp": b + 1 - 2 * lax.rem(b, 2)}
    rows, d = x.shape
    half, fq = w1.shape
    sub = rows // 4
    c1 = fq // N1
    c2 = half // N2
    cb = c1 // 2
    fr = NR * c1
    t0 = fr - c1
    kr = 2 * fr
    ke = 4 * c1
    wide = half // 2
    piece = rows // NX
    near = pl.multiple_of(a * half, half)
    away = pl.multiple_of((1 - a) * half, half)
    everything = slice(None)

    def remote(src, dst, ssem, rsem, to):
        return pltpu.make_async_remote_copy(
            src_ref=src, dst_ref=dst, send_sem=ssem, recv_sem=rsem, device_id=to, device_id_type=MESH
        )

    def cols1(j):
        return (everything, pl.ds(pl.multiple_of(j * c1, c1), c1))

    def cols2(k):
        return pl.ds(pl.multiple_of(k * c2, c2), c2)

    def w1_y(j):
        return remote(w1.at[cols1(j)], w1far.at[cols1(j)], w1y_s.at[j], w1y_r.at[j], to_y)

    def w1_ye():
        return remote(w1e, w1far.at[cols1(N1)], w1y_s.at[N1], w1y_r.at[N1], to_y)

    def w1_yr(j):
        return remote(w1far.at[cols1(j)], w1far.at[cols1(j)], w1y_s.at[j], w1y_r.at[j], to_y)

    def w1_c(j):
        return remote(w1.at[cols1(j)], w1so.at[cols1(j)], w1c_s.at[j], w1c_r.at[j], to_c)

    def w1_ce():
        return remote(w1e, w1so.at[cols1(N1)], w1c_s.at[N1], w1c_r.at[N1], to_c)

    def w1_cr(j):
        return remote(w1so.at[cols1(j)], w1so.at[cols1(j)], w1c_s.at[j], w1c_r.at[j], to_c)

    def w1_f(j):
        return remote(w1far.at[cols1(j)], w1sf.at[cols1(j)], w1f_s.at[j], w1f_r.at[j], to_c)

    def cols_t(t):
        return (everything, pl.ds(t0 + t * cb, cb))

    def tail_at(t):
        return NR - 1 if t == 0 else N1 + 1

    def w1_yt(t):
        return remote(w1.at[cols_t(t)], w1far.at[cols_t(t)], w1y_s.at[tail_at(t)], w1y_r.at[tail_at(t)], to_y)

    def w1_ft(t):
        return remote(w1far.at[cols_t(t)], w1sf.at[cols_t(t)], w1f_s.at[tail_at(t)], w1f_r.at[tail_at(t)], to_c)

    def w1_e():
        return remote(w1.at[cols1(N1 - 1)], w1e, e_s.at[0], e_r.at[0], to_x)

    def w2_e():
        return remote(w2.at[fr:fq], w2e, e_s.at[1], e_r.at[1], to_x)

    def w2_yf(k):
        at = (pl.ds(0, fr), cols2(k))
        return remote(w2.at[at], w2far.at[at], w2y_s.at[k], w2y_r.at[k], to_y)

    def w2_yg(g):
        at = (pl.ds(fr, c1), pl.ds(g * wide, wide))
        to = (pl.ds(fq, c1), pl.ds(g * wide, wide))
        return (
            remote(w2.at[at], w2far.at[at], w2y_s.at[N2 + 2 * g], w2y_r.at[N2 + 2 * g], to_y),
            remote(
                w2e.at[:, pl.ds(g * wide, wide)], w2far.at[to], w2y_s.at[N2 + 2 * g + 1], w2y_r.at[N2 + 2 * g + 1], to_y
            ),
        )

    def w2_c(k):
        at = (everything, cols2(k))
        return remote(w2.at[at], w2so.at[pl.ds(0, fq), cols2(k)], w2c_s.at[k], w2c_r.at[k], to_c)

    def w2_ce():
        return remote(w2e, w2so.at[fq : fq + c1], w2c_s.at[N2], w2c_r.at[N2], to_c)

    def w2_ff(k):
        at = (pl.ds(0, fr), cols2(k))
        return remote(w2far.at[at], w2sf.at[at], w2f_s.at[k], w2f_r.at[k], to_c)

    def w2_fg(g):
        at = (pl.ds(fr, 2 * c1), pl.ds(g * wide, wide))
        return remote(w2far.at[at], w2sf.at[at], w2f_s.at[N2 + g], w2f_r.at[N2 + g], to_c)

    def xrows(t):
        return pl.ds(pl.multiple_of(t * piece, piece), piece)

    def xn_x(t):
        return remote(xn.at[xrows(t)], xn.at[xrows(t + NX)], xn_s.at[t], xn_r.at[t], to_x)

    def p_x(i, k):
        at = (pl.ds(pl.multiple_of(i * sub, sub), sub), cols2(k))
        return remote(psend.at[at], precv.at[at], p_s.at[k * 4 + i], p_r.at[k * 4 + i], to_x)

    barrier = pltpu.get_barrier_semaphore()
    for to in (to_y, to_x, to_c):
        pl.semaphore_signal(barrier, inc=1, device_id=to, device_id_type=MESH)
    pl.semaphore_wait(barrier, 3)

    for j in range(AHEAD):
        w1_y(j).start()

    @pl.loop(0, N1)
    def _(j):
        w1_c(j).start()

    def gam_in():
        return [
            pltpu.make_async_copy(gamma.at[:, pl.ds(off, half)], gam.at[:, i * half : (i + 1) * half], io_sem.at[i])
            for i, off in enumerate((near, away))
        ]

    def x_in(t, slot):
        return [
            pltpu.make_async_copy(
                x.at[xrows(t), pl.ds(off, half)],
                act.at[slot, 0:piece, i * half : (i + 1) * half],
                act_sem.at[slot, i],
            )
            for i, off in enumerate((near, away))
        ]

    for c in gam_in():
        c.start()
    for c in x_in(0, 0):
        c.start()
    for c in gam_in():
        c.wait()

    @pl.loop(0, NX)
    def _(t):
        slot = t % 2

        @pl.when(t + 1 < NX)
        def _():
            for c in x_in(t + 1, 1 - slot):
                c.start()

        for c in x_in(t, slot):
            c.wait()

        @pl.loop(0, piece // 16)
        def _(r):
            at = pl.multiple_of(r * 16, 16)
            xs = act[slot, pl.ds(at, 16), 0:d].astype(F32)
            xc = xs - jnp.mean(xs, axis=1, keepdims=True)
            var = jnp.mean(xc * xc, axis=1, keepdims=True)
            act[slot, pl.ds(piece + at, 16), 0:d] = (xc * lax.rsqrt(var + EPS) * gam[...]).astype(BF16)

        out = pltpu.make_async_copy(act.at[slot, piece : 2 * piece, 0:d], xn.at[xrows(t)], io_sem.at[2])
        out.start()
        out.wait()

        @pl.when(t < NX // 2)
        def _():
            xn_x(t).start()

    def hcol(j, q):
        return pl.multiple_of(_where(j < NR, q * fr + j * c1, kr + (j - NR) * 2 * c1 + q * c1), c1)

    def tile_rows(m):
        return _where(m < 3, 2 * m, 3 + m), m < 3

    def hrows(r):
        return pl.ds(pl.multiple_of(r * sub, sub), sub)

    def a1_in(m, slot, go):
        r0, two = tile_rows(m)

        def one(i):
            c = pltpu.make_async_copy(
                xn.at[hrows(r0 + i)], act.at[slot, :, i * d : (i + 1) * d], act_sem.at[slot, i]
            )
            c.start() if go else c.wait()

        one(0)
        pl.when(two)(lambda: one(1))

    def w1_in(j, q, slot, go):
        def load(i, ref, at):
            c = pltpu.make_async_copy(ref.at[at], wb.at[slot, i * half : (i + 1) * half], w_sem.at[slot, i])
            c.start() if go else c.wait()

        if not go:
            for i in range(2):
                load(i, w1far, cols1(j))
            return
        pl.when((q == 0) & (j < N1))(lambda: load(0, w1, cols1(j)))
        pl.when((q == 0) & (j == N1))(lambda: load(0, w1e, (everything, everything)))
        pl.when(q == 0)(lambda: load(1, w1far, cols1(j)))

        @pl.when(q == 1)
        def _():
            load(0, w1so, cols1(j))
            load(1, w1sf, cols1(j))

    starts1, total1 = _bounds1()
    first2, first3, first4 = (
        next(at for at, (_, (m0, nm)) in zip(starts1, STEPS1) if m0 == m) for m in (2, 3, 4)
    )

    def arrive1(s):
        j, q, m = _step1(s)
        first = m == _first_tile(j)

        @pl.when(first & (q == 0))
        def _():
            w1_yr(j).wait_recv()
            w1_f(j).start()

            @pl.when(j + AHEAD < NR - 1)
            def _():
                w1_y(j + AHEAD).start()

            @pl.when(j + AHEAD == NR - 1)
            def _():
                w1_yt(0).start()
                w1_yt(1).start()
                w1_e().start()
                w2_e().start()

            @pl.when(j == 2)
            def _():
                for t in range(NX // 2, NX):
                    xn_x(t).start()

            @pl.when(j == 4)
            def _():
                for k in range(N2):
                    w2_c(k).start()

        @pl.when(first & (q == 1))
        def _():
            w1_cr(j).wait_recv()
            w1_f(j).wait_recv()

        for at, lo, hi in ((first2, 0, 4), (first3, 4, 6), (first4, 6, 8)):

            @pl.when(s == at)
            def _():
                for t in range(lo, hi):
                    xn_x(t).wait_recv()

    def load1(s, aslot, wslot, a_new, w_new):
        j, q, m = _step1(s)
        pl.when(a_new)(lambda: a1_in(m, aslot, True))
        pl.when(w_new)(lambda: w1_in(j, q, wslot, True))

    def h_out(s, i):
        j, q, m = _step1(s)
        r0, _ = tile_rows(m)
        return pltpu.make_async_copy(
            hout.at[s % 2, pl.ds(pl.multiple_of(i * sub, sub), sub)],
            h.at[hrows(r0 + i), pl.ds(hcol(j, q), c1)],
            h_sem.at[s % 2, i],
        )

    def h_done(s):
        _, two = tile_rows(_step1(s)[2])
        h_out(s, 0).wait()
        pl.when(two)(lambda: h_out(s, 1).wait())

    def first_product(lo, hi):
        arrive1(lo)
        load1(lo, 0, 0, True, True)

        def step(s, carry):
            aslot, wslot, a_fresh, w_fresh = carry
            j, q, m = _step1(s)
            nj, nq, nm = _step1(s + 1)
            more = s + 1 < hi
            a_new = more & (nm != m)
            w_new = more & ((nj != j) | (nq != q))
            na = _where(a_new, 1 - aslot, aslot)
            nw = _where(w_new, 1 - wslot, wslot)
            pl.when(more)(lambda: arrive1(s + 1))
            load1(s + 1, na, nw, a_new, w_new)
            pl.when(a_fresh == 1)(lambda: a1_in(m, aslot, False))
            pl.when(w_fresh == 1)(lambda: w1_in(j, q, wslot, False))
            pl.when(s >= lo + 2)(lambda: h_done(s - 2))
            _, two = tile_rows(m)

            @pl.loop(0, _where(two, 2, 1))
            def _(i):
                u = jnp.dot(
                    act[aslot, :, pl.ds(pl.multiple_of(i * d, d), d)], wb[wslot, 0:d], preferred_element_type=F32
                )
                hout[s % 2, pl.ds(pl.multiple_of(i * sub, sub), sub)] = jax.nn.gelu(u, approximate=True).astype(BF16)
                h_out(s, i).start()

            return na, nw, _where(a_new, 1, 0), _where(w_new, 1, 0)

        one, nil = jnp.int32(1), jnp.int32(0)
        lax.fori_loop(lo, hi, step, (nil, nil, one, one))
        h_done(hi - 2)
        h_done(hi - 1)

    def a2_in(typ, k, i, slot, go):
        r = _where(typ == REM, 4, 0) + i

        def wait_or_start(c):
            c.start() if go else c.wait()

        @pl.when(typ != END)
        def _():
            wait_or_start(pltpu.make_async_copy(h.at[hrows(r), 0:kr], act.at[slot, :, 0:kr], act_sem.at[slot, 0]))

        @pl.when(typ == END)
        def _():
            wait_or_start(
                pltpu.make_async_copy(h.at[hrows(r), kr : kr + ke], act.at[slot, :, 0:ke], act_sem.at[slot, 0])
            )
            ycol = pl.multiple_of(_where(k < N2, near, away) + (k % N2) * c2, c2)
            wait_or_start(pltpu.make_async_copy(pown.at[hrows(i), cols2(k)], pback.at[slot], in_sem.at[slot, 0]))
            wait_or_start(pltpu.make_async_copy(x.at[hrows(i), pl.ds(ycol, c2)], xin.at[slot], in_sem.at[slot, 1]))

    def w2_in(typ, k, slot, go):
        def load(n, at, rows_, ref, from_, kk):
            c = pltpu.make_async_copy(
                ref.at[pl.ds(from_, rows_), cols2(kk)], wb.at[slot, at : at + rows_], w_sem.at[slot, n]
            )
            c.start() if go else c.wait()

        def main(own, sib, kk):
            load(0, 0, fr, own, 0, kk)
            load(1, fr, fr, sib, 0, kk)

        def rest(own, ext, ext_at, sib, kk):
            load(0, 0, c1, own, fr, kk)
            load(1, c1, c1, sib, fr, kk)
            load(2, 2 * c1, c1, ext, ext_at, kk)
            load(3, 3 * c1, c1, sib, fq, kk)

        def both(side, kk, own, ext, ext_at, sib):
            pl.when(side & (typ != END))(lambda: main(own, sib, kk))
            pl.when(side & (typ == END))(lambda: rest(own, ext, ext_at, sib, kk))

        if not go:
            pl.when(typ != END)(lambda: main(w2far, w2sf, 0))
            pl.when(typ == END)(lambda: rest(w2far, w2far, fq, w2sf, 0))
            return
        both(k < N2, k, w2, w2e, 0, w2so)
        both(k >= N2, k - N2, w2far, w2far, fq, w2sf)

    def arrive2(v):
        at = {visit: n for n, visit in enumerate(VISITS)}
        for n in range(len(VISITS)):
            visit = VISITS[n]
            todo = []
            for u in SEND_F.get(visit, ()):
                todo.append(lambda u=u: w2_yf(u).start())
            if visit in SEND_G:
                todo.append(lambda g=SEND_G[visit]: [c.start() for c in w2_yg(g)])
            if visit in PASS_F:
                u = PASS_F[visit]
                todo.append(lambda u=u: (w2_yf(u).wait_recv(), w2_ff(u).start()))
            if visit in PASS_G:
                g = PASS_G[visit]
                todo.append(lambda g=g: ([c.wait_recv() for c in w2_yg(g)], w2_fg(g).start()))
            if visit[0] == REM:
                k = visit[1]
                todo.append(lambda k=k: w2_c(k).wait_recv() if k < N2 else w2_ff(k - N2).wait_recv())
            if n == min(at[B(k)] for k in range(N2)):
                todo.append(lambda: w2_ce().wait_recv())
            for g in range(2):
                if n == min(at[B(N2 + 3 * g + k)] for k in range(3)):
                    todo.append(lambda g=g: w2_fg(g).wait_recv())
            if todo:

                @pl.when(v == n)
                def _(todo=todo):
                    for f in todo:
                        f()

    def p_out(to, k, i, slot):
        return pltpu.make_async_copy(pout.at[slot], to.at[hrows(i), cols2(k)], out_sem.at[slot])

    def y_out(k, i, slot):
        ycol = pl.multiple_of(_where(k < N2, near, away) + (k % N2) * c2, c2)
        return pltpu.make_async_copy(yout.at[slot], y.at[hrows(i), pl.ds(ycol, c2)], out_sem.at[2 + slot])

    def finish(typ, k, i, slot):
        @pl.when((typ == REM) | (typ == OWN))
        def _():
            p_out(pown, k, i, slot).wait()

        @pl.when(typ == REM)
        def _():
            p_x(i, k).start()

        @pl.when(typ == END)
        def _():
            y_out(k, i, slot).wait()

    def second_product(lo, hi):
        arrive2(lo)
        typ0, k0 = _visit(lo)
        w2_in(typ0, k0, 0, True)
        a2_in(typ0, k0, jnp.int32(0), 0, True)

        def visit(v, carry):
            typ, k, ptyp, pk = carry
            more = v + 1 < hi
            ntyp, nk = _visit(v + 1)
            wslot = (v - lo) % 2

            def tile(i, before):
                btyp, bk, bi = before
                slot = i % 2
                last = i == 3

                @pl.when(last & more)
                def _():
                    arrive2(v + 1)
                    w2_in(ntyp, nk, 1 - wslot, True)

                @pl.when(more | (i < 3))
                def _():
                    a2_in(_where(last, ntyp, typ), _where(last, nk, k), _where(last, 0, i + 1), 1 - slot, True)

                a2_in(typ, k, i, slot, False)
                pl.when(i == 0)(lambda: w2_in(typ, k, wslot, False))

                @pl.when(typ != END)
                def _():
                    pout[slot] = jnp.dot(act[slot, :, 0:kr], wb[wslot, 0:kr], preferred_element_type=F32)

                @pl.when(typ == END)
                def _():
                    pout[slot] = jnp.dot(act[slot, :, 0:ke], wb[wslot, 0:ke], preferred_element_type=F32)

                finish(btyp, bk, bi, 1 - slot)
                pl.when(typ == OWN)(lambda: p_out(pown, k, i, slot).start())
                pl.when(typ == REM)(lambda: p_out(psend, k, i, slot).start())

                @pl.when(typ == END)
                def _():
                    p_x(i, k).wait_recv()
                    got = pltpu.make_async_copy(precv.at[hrows(i), cols2(k)], pin, io_sem.at[0])
                    got.start()
                    got.wait()
                    total = (pback[slot] + pout[slot]) + pin[...]
                    yout[slot] = (xin[slot].astype(F32) + total).astype(BF16)
                    y_out(k, i, slot).start()

                return typ, k, i

            ptyp, pk, _ = lax.fori_loop(0, 4, tile, (ptyp, pk, jnp.int32(3)))
            return ntyp, nk, ptyp, pk

        _, _, ptyp, pk = lax.fori_loop(lo, hi, visit, (typ0, k0, jnp.int32(3), jnp.int32(0)))
        finish(ptyp, pk, jnp.int32(3), 1)

    def junction():
        def w_tail(t, part):
            refs = ((w1, w1so), (w1far, w1sf))[part]
            return [
                pltpu.make_async_copy(
                    refs[q].at[cols_t(t)],
                    wb.at[0, t * d + part * half : t * d + (part + 1) * half, q * cb : (q + 1) * cb],
                    tail_sem.at[t, part, q],
                )
                for q in range(2)
            ]

        def xn_in(i):
            return pltpu.make_async_copy(xn.at[hrows(4 + i)], act.at[1, :, 0:d], act_sem.at[1, 0])

        def h_at(i, q, col, width):
            return h.at[hrows(4 + i), q * fr + col : q * fr + col + width]

        def h_in(i):
            return [
                pltpu.make_async_copy(h_at(i, q, 0, t0), act.at[0, :, q * fr : q * fr + t0], act_sem.at[0, q])
                for q in range(2)
            ]

        def arrive(t):
            w1_yt(t).wait_recv()
            w1_ft(t).start()
            if t == 1:
                w1_y(N1 - 1).start()
                w1_e().wait_recv()
                w1_ye().start()
                w2_yf(0).start()
                w2_yf(1).start()
                w2_e().wait_recv()
            w1_ft(t).wait_recv()
            for c in w_tail(t, 1):
                c.start()
            if t == 1:
                w1_ce().start()
                w2_ce().start()
            for part in range(2):
                for c in w_tail(t, part):
                    c.wait()

        w1_c(NR - 1).wait_recv()
        for t in range(2):
            for c in w_tail(t, 0):
                c.start()
        xn_in(0).start()
        for c in h_in(0):
            c.start()
        w2_c(0).wait_recv()
        rem, zero = jnp.int32(REM), jnp.int32(0)
        w2_in(rem, zero, 1, True)
        arrive(0)
        w2_in(rem, zero, 1, False)

        def tile_(i, carry):
            xn_in(i).wait()
            u = jnp.dot(act[1, :, 0:d], wb[0, 0:d], preferred_element_type=F32)
            g = jax.nn.gelu(u, approximate=True).astype(BF16)
            for c in h_in(i):
                c.wait()
            first = []
            for q in range(2):
                at = q * fr + t0
                act[0, :, at : at + cb] = g[:, q * cb : (q + 1) * cb]
                first.append(pltpu.make_async_copy(act.at[0, :, at : at + cb], h_at(i, q, t0, cb), h_sem.at[0, q]))
                first[-1].start()
            n = fr - cb
            pout[0] = jnp.dot(act[0, :, 0:n], wb[1, 0:n], preferred_element_type=F32) + jnp.dot(
                act[0, :, fr : fr + n], wb[1, fr : fr + n], preferred_element_type=F32
            )
            for c in first:
                c.wait()

            @pl.when(i < 3)
            def _():
                for c in h_in(i + 1):
                    c.start()

            pl.when(i == 0)(lambda: arrive(1))
            u = jnp.dot(act[1, :, 0:d], wb[0, d : 2 * d], preferred_element_type=F32)
            hout[0, 0:sub] = jax.nn.gelu(u, approximate=True).astype(BF16)
            pl.when(i < 3)(lambda: xn_in(i + 1).start())
            second = []
            for q in range(2):
                second.append(
                    pltpu.make_async_copy(
                        hout.at[0, 0:sub, q * cb : (q + 1) * cb], h_at(i, q, t0 + cb, cb), h_sem.at[1, q]
                    )
                )
                second[-1].start()
            pout[0] += jnp.dot(hout[0, 0:sub, 0:cb], wb[1, n:fr], preferred_element_type=F32) + jnp.dot(
                hout[0, 0:sub, cb : 2 * cb], wb[1, fr + n : kr], preferred_element_type=F32
            )
            out = p_out(psend, zero, i, 0)
            out.start()
            out.wait()
            p_x(i, 0).start()
            for c in second:
                c.wait()
            return carry

        lax.fori_loop(0, 4, tile_, jnp.int32(0))

    @pl.loop(0, 2)
    def _(phase):
        early = phase == 0
        cut = starts1[BREAK1]
        first_product(_where(early, 0, cut), _where(early, cut, total1))
        pl.when(early)(junction)
        second_product(_where(early, 0, BREAK2), _where(early, BREAK2, len(VISITS)))

    @pl.loop(0, N1 + 1)
    def _(j):
        w1_cr(j).wait_send()

    @pl.loop(0, N1 + 1)
    def _(j):
        @pl.when(j != NR - 1)
        def _():
            w1_yr(j).wait_send()
            w1_f(j).wait_send()

    for t in range(2):
        w1_yt(t).wait_send()
        w1_ft(t).wait_send()

    @pl.loop(0, N2)
    def _(k):
        w2_yf(k).wait_send()
        w2_c(k).wait_send()
        w2_ff(k).wait_send()

    w1_e().wait_send()
    w2_e().wait_send()
    w2_ce().wait_send()
    for g in range(2):
        for c in w2_yg(g):
            c.wait_send()
        w2_fg(g).wait_send()

    @pl.loop(0, NX)
    def _(t):
        xn_x(t).wait_send()

    @pl.loop(0, 2 * N2 * 4)
    def _(s):
        p_x(s % 4, s // 4).wait_send()


PUTS = 16


def _put(src, dst, buf, sems_in, sems_out):
    n = src.shape[0] // PUTS

    def get(i):
        return pltpu.make_async_copy(src.at[i * n : (i + 1) * n], buf.at[i], sems_in.at[i])

    def put(i):
        return pltpu.make_async_copy(buf.at[i], dst.at[i * n : (i + 1) * n], sems_out.at[i])

    for i in range(PUTS):
        get(i).start()
    for i in range(PUTS):
        get(i).wait()
        put(i).start()
    for i in range(PUTS):
        put(i).wait()


def solution(mesh):
    def body(x, gamma, w1, w2):
        rows, d = x.shape
        half, fq = w1.shape
        sub = rows // 4
        c1, c2 = fq // N1, half // N2

        def hbm(*shape, dtype=BF16):
            return jax.ShapeDtypeStruct(shape, dtype)

        dma = pltpu.SemaphoreType.DMA
        outs = (
            hbm(rows, d),
            hbm(2 * rows, d),
            hbm(half, c1), hbm(half, fq + c1), hbm(half, fq + c1), hbm(half, fq + c1),
            hbm(c1, half), hbm(fq + c1, half), hbm(fq + c1, half), hbm(fq + c1, half),
            hbm(2 * rows, 2 * (fq + c1)),
            hbm(rows, d, dtype=F32), hbm(rows, d, dtype=F32), hbm(rows, d, dtype=F32),
        )
        out = pl.pallas_call(
            _kernel,
            name="mlp",
            out_shape=outs,
            in_specs=[pl.BlockSpec(memory_space=pl.ANY)] * 4,
            out_specs=tuple([pl.BlockSpec(memory_space=pl.ANY)] * len(outs)),
            scratch_shapes=[
                pltpu.VMEM((2, sub, 2 * d), BF16),
                pltpu.VMEM((2, 2 * fq, c2), BF16),
                pltpu.VMEM((2, 2 * sub, c1), BF16),
                pltpu.VMEM((2, sub, c2), F32),
                pltpu.VMEM((sub, c2), F32),
                pltpu.VMEM((2, sub, c2), F32),
                pltpu.VMEM((2, sub, c2), BF16),
                pltpu.VMEM((2, sub, c2), BF16),
                pltpu.VMEM((1, d), F32),
                dma((2, 2)), dma((2, 4)), dma((2, 2)), dma((3,)), dma((4,)), dma((2, 2)), dma((2, 2, 2)),
                dma((NX,)), dma((NX,)), dma((2,)), dma((2,)),
                dma((N1 + 2,)), dma((N1 + 2,)), dma((N1 + 1,)), dma((N1 + 1,)), dma((N1 + 2,)), dma((N1 + 2,)),
                dma((N2 + 4,)), dma((N2 + 4,)), dma((N2 + 1,)), dma((N2 + 1,)), dma((N2 + 2,)), dma((N2 + 2,)),
                dma((8 * N2,)), dma((8 * N2,)),
            ],
            compiler_params=pltpu.CompilerParams(
                collective_id=0, has_side_effects=True, vmem_limit_bytes=67_000_000
            ),
        )(x, gamma.reshape(1, d), w1, w2)
        return pl.pallas_call(
            _put,
            name="put",
            out_shape=hbm(rows, d),
            in_specs=[pl.BlockSpec(memory_space=pl.ANY)],
            out_specs=pl.BlockSpec(memory_space=pl.ANY),
            scratch_shapes=[pltpu.VMEM((PUTS, rows // PUTS, d), BF16), dma((PUTS,)), dma((PUTS,))],
            compiler_params=pltpu.CompilerParams(vmem_limit_bytes=40_000_000),
        )(out[0])

    return jax.shard_map(
        body,
        mesh=mesh,
        in_specs=(P(("fsdp", "tp"), None), P(None), P("fsdp", "tp"), P("tp", "fsdp")),
        out_specs=P(("fsdp", "tp"), None),
        check_vma=False,
    )
```

time: 4330 us -> 1890 us (0.44)
  waiting for transfers between devices: 2890 us -> 0 us
  Pallas kernels: 0 us -> 1890 us
  matrix products: 1360 us -> 0 us
  other arithmetic: 77.1 us -> 0 us
    pallas_call x0 -> x2, Pallas kernels: none -> 1890 us  [the longest x1 1870 us: body(): pl.pallas_call(_kernel, name='mlp', out_shape=outs, in_specs=[pl.BlockSpe...]
    all_gather x3 -> x0, waiting for transfers between devices: 1620 us -> none  [the longest x1 816 us: body(): w1f = lax.all_gather(w1, 'fsdp', axis=0, tiled=True)]
    dot_general x2 -> x0, matrix products: 1360 us -> none  [the longest x1 713 us: body(): yp = jnp.dot(h, w2f, preferred_element_type=jnp.float32)]
    reduce_scatter x1 -> x0, waiting for transfers between devices: 1270 us -> none  [body(): y = lax.psum_scatter(yp, 'tp', scatter_dimension=0, tiled=True)]
    convert_element_type x2 -> x0, other arithmetic: 55.8 us -> none  [the longest x1 32.4 us: body(): return (xf + y).astype(jnp.bfloat16)]
  transfers between devices with their start and end apart: 4 -> 0, of which waited for: 4 -> 0; matrix products, arithmetic and copies ran while one was open for 16% -> 0% of each run, Pallas kernels for 0% -> 0%
where the time goes in v3:
time: 1890 us
  Pallas kernels  1890 us (100%)
    pallas_call x1, Pallas kernels, body(): pl.pallas_call(_kernel, name='mlp', out_shape=outs, in_specs=[pl.BlockSpe...  1870 us

profile of v3, /device:TPU:0, one launch (start us, length us, event | category | flops | bytes accessed | tf_op | source)
XLA Modules:
  0.0 1887.2 jit_solution(9860433202313068775)
XLA Ops:
  0.0 1869.9 %mlp.1 = (bf16[2048,6144]{1,0:T(8,128)(2,1)}, bf16[4096,6144]{1,0:T(8,128)(2,1)}, bf16[3072,512]{1,0:T(8,128)(2,1)}, bf16[3072,6656]{1,0:T(8,128)(2,1)}, bf16[30...) custom-call(bf16[2048,6144]{1,0:T(8,128)(2,1)} %x.1, ...), custom_call_target="tpu_custom_call" | custom-call | tf_op jit(solution)/shard_map/mlp/pallas_call | solution.py:752
  1869.9 17.3 put.1

commit v4 on v3

--- a/solution.py
+++ b/solution.py
@@ -20,18 +20,19 @@
     ((0, 4), (0, 2)),
     ((0, 4), (2, 1)),
     ((4, 2), (0, 3)),
-    ((0, 3), (3, 1)),
+    ((0, 3), (4, 1)),
     ((6, 1), (0, 3)),
-    ((3, 4), (3, 1)),
-    ((7, 1), (2, 2)),
-    ((0, 8), (4, 1)),
-    ((7, 1), (0, 2)),
-    ((8, 2), (2, 3)),
-    ((8, 5), (0, 2)),
+    ((3, 4), (4, 1)),
+    ((7, 1), (2, 1)),
+    ((7, 1), (4, 1)),
+    ((0, 8), (5, 1)),
+    ((8, 2), (2, 2)),
+    ((7, 6), (0, 2)),
 )
 BREAK1 = 10
 
 REM, OWN, END = 0, 1, 2
+LAST = 2 * N2 - 1
 R, A, B = ((lambda k, t=t: (t, k)) for t in (REM, OWN, END))
 VISITS = (
     R(1), R(2), R(3), R(4),
@@ -43,6 +44,10 @@
 PASS_G = {B(4): 0, A(11): 1}
 SEND_F = {R(2): (2,), R(5): (3, 4), R(7): (5,)}
 SEND_G = {R(2): 0, R(7): 1}
+
+
+def _tail(c1):
+    return ((0, c1 // 2), (c1 // 2, c1 // 2))
 
 
 def _where(cond, a, b):
@@ -98,7 +103,7 @@
     sub = rows // 4
     c1 = fq // N1
     c2 = half // N2
-    cb = c1 // 2
+    tail = _tail(c1)
     fr = NR * c1
     t0 = fr - c1
     kr = 2 * fr
@@ -142,10 +147,10 @@
         return remote(w1far.at[cols1(j)], w1sf.at[cols1(j)], w1f_s.at[j], w1f_r.at[j], to_c)
 
     def cols_t(t):
-        return (everything, pl.ds(t0 + t * cb, cb))
+        return (everything, pl.ds(t0 + tail[t][0], tail[t][1]))
 
     def tail_at(t):
-        return NR - 1 if t == 0 else N1 + 1
+        return NR - 1 if t == 0 else N1 + t
 
     def w1_yt(t):
         return remote(w1.at[cols_t(t)], w1far.at[cols_t(t)], w1y_s.at[tail_at(t)], w1y_r.at[tail_at(t)], to_y)
@@ -265,7 +270,7 @@
         return pl.multiple_of(_where(j < NR, q * fr + j * c1, kr + (j - NR) * 2 * c1 + q * c1), c1)
 
     def tile_rows(m):
-        return _where(m < 3, 2 * m, 3 + m), m < 3
+        return _where(m < 4, 2 * m, 2 + m), m < 4
 
     def hrows(r):
         return pl.ds(pl.multiple_of(r * sub, sub), sub)
@@ -302,7 +307,7 @@
 
     starts1, total1 = _bounds1()
     first2, first3, first4 = (
-        next(at for at, (_, (m0, nm)) in zip(starts1, STEPS1) if m0 == m) for m in (2, 3, 4)
+        next(at for at, (_, (m0, nm)) in zip(starts1, STEPS1) if m0 == m) for m in (2, 4, 5)
     )
 
     def arrive1(s):
@@ -320,8 +325,8 @@
 
             @pl.when(j + AHEAD == NR - 1)
             def _():
-                w1_yt(0).start()
-                w1_yt(1).start()
+                for t in range(len(tail)):
+                    w1_yt(t).start()
                 w1_e().start()
                 w2_e().start()
 
@@ -401,6 +406,9 @@
         h_done(hi - 2)
         h_done(hi - 1)
 
+    def p_in(i, k, slot):
+        return pltpu.make_async_copy(precv.at[hrows(i), cols2(k)], pin.at[slot], in_sem.at[slot, 2])
+
     def a2_in(typ, k, i, slot, go):
         r = _where(typ == REM, 4, 0) + i
 
@@ -419,6 +427,12 @@
             ycol = pl.multiple_of(_where(k < N2, near, away) + (k % N2) * c2, c2)
             wait_or_start(pltpu.make_async_copy(pown.at[hrows(i), cols2(k)], pback.at[slot], in_sem.at[slot, 0]))
             wait_or_start(pltpu.make_async_copy(x.at[hrows(i), pl.ds(ycol, c2)], xin.at[slot], in_sem.at[slot, 1]))
+            if go:
+
+                @pl.when(k < LAST)
+                def _():
+                    p_x(i, k).wait_recv()
+                    p_in(i, k, slot).start()
 
     def w2_in(typ, k, slot, go):
         def load(n, at, rows_, ref, from_, kk):
@@ -481,9 +495,9 @@
     def p_out(to, k, i, slot):
         return pltpu.make_async_copy(pout.at[slot], to.at[hrows(i), cols2(k)], out_sem.at[slot])
 
-    def y_out(k, i, slot):
+    def y_out(k, i):
         ycol = pl.multiple_of(_where(k < N2, near, away) + (k % N2) * c2, c2)
-        return pltpu.make_async_copy(yout.at[slot], y.at[hrows(i), pl.ds(ycol, c2)], out_sem.at[2 + slot])
+        return pltpu.make_async_copy(yout, y.at[hrows(i), pl.ds(ycol, c2)], out_sem.at[2])
 
     def finish(typ, k, i, slot):
         @pl.when((typ == REM) | (typ == OWN))
@@ -496,7 +510,7 @@
 
         @pl.when(typ == END)
         def _():
-            y_out(k, i, slot).wait()
+            y_out(k, i).wait()
 
     def second_product(lo, hi):
         arrive2(lo)
@@ -541,13 +555,15 @@
 
                 @pl.when(typ == END)
                 def _():
-                    p_x(i, k).wait_recv()
-                    got = pltpu.make_async_copy(precv.at[hrows(i), cols2(k)], pin, io_sem.at[0])
-                    got.start()
-                    got.wait()
-                    total = (pback[slot] + pout[slot]) + pin[...]
-                    yout[slot] = (xin[slot].astype(F32) + total).astype(BF16)
-                    y_out(k, i, slot).start()
+                    @pl.when(k == LAST)
+                    def _():
+                        p_x(i, k).wait_recv()
+                        p_in(i, k, slot).start()
+
+                    p_in(i, k, slot).wait()
+                    total = (pback[slot] + pout[slot]) + pin[slot]
+                    yout[...] = (xin[slot].astype(F32) + total).astype(BF16)
+                    y_out(k, i).start()
 
                 return typ, k, i
 
@@ -558,12 +574,20 @@
         finish(ptyp, pk, jnp.int32(3), 1)
 
     def junction():
+        final = len(tail) - 1
+
+        def lanes(t):
+            at = 0 if t < 2 else 2 * sum(w for _, w in tail[1:t])
+            return (0 if t == 0 else d), at
+
         def w_tail(t, part):
             refs = ((w1, w1so), (w1far, w1sf))[part]
+            r, at = lanes(t)
+            w = tail[t][1]
             return [
                 pltpu.make_async_copy(
                     refs[q].at[cols_t(t)],
-                    wb.at[0, t * d + part * half : t * d + (part + 1) * half, q * cb : (q + 1) * cb],
+                    wb.at[0, r + part * half : r + (part + 1) * half, at + q * w : at + (q + 1) * w],
                     tail_sem.at[t, part, q],
                 )
                 for q in range(2)
@@ -581,10 +605,15 @@
                 for q in range(2)
             ]
 
+        def hidden(t):
+            r, at = lanes(t)
+            u = jnp.dot(act[1, :, 0:d], wb[0, r : r + d, at : at + 2 * tail[t][1]], preferred_element_type=F32)
+            return jax.nn.gelu(u, approximate=True).astype(BF16)
+
         def arrive(t):
             w1_yt(t).wait_recv()
             w1_ft(t).start()
-            if t == 1:
+            if t == final:
                 w1_y(N1 - 1).start()
                 w1_e().wait_recv()
                 w1_ye().start()
@@ -594,7 +623,7 @@
             w1_ft(t).wait_recv()
             for c in w_tail(t, 1):
                 c.start()
-            if t == 1:
+            if t == final:
                 w1_ce().start()
                 w2_ce().start()
             for part in range(2):
@@ -602,7 +631,7 @@
                     c.wait()
 
         w1_c(NR - 1).wait_recv()
-        for t in range(2):
+        for t in range(len(tail)):
             for c in w_tail(t, 0):
                 c.start()
         xn_in(0).start()
@@ -616,21 +645,28 @@
 
         def tile_(i, carry):
             xn_in(i).wait()
-            u = jnp.dot(act[1, :, 0:d], wb[0, 0:d], preferred_element_type=F32)
-            g = jax.nn.gelu(u, approximate=True).astype(BF16)
-            for c in h_in(i):
-                c.wait()
-            first = []
-            for q in range(2):
-                at = q * fr + t0
-                act[0, :, at : at + cb] = g[:, q * cb : (q + 1) * cb]
-                first.append(pltpu.make_async_copy(act.at[0, :, at : at + cb], h_at(i, q, t0, cb), h_sem.at[0, q]))
-                first[-1].start()
-            n = fr - cb
+            out = []
+            for t in range(final):
+                if t > 0:
+                    pl.when(i == 0)(lambda t=t: arrive(t))
+                g = hidden(t)
+                if t == 0:
+                    for c in h_in(i):
+                        c.wait()
+                off, w = tail[t]
+                for q in range(2):
+                    at = q * fr + t0 + off
+                    act[0, :, at : at + w] = g[:, q * w : (q + 1) * w]
+                    out.append(
+                        pltpu.make_async_copy(act.at[0, :, at : at + w], h_at(i, q, t0 + off, w), h_sem.at[t, q])
+                    )
+                    out[-1].start()
+            off, w = tail[final]
+            n = fr - w
             pout[0] = jnp.dot(act[0, :, 0:n], wb[1, 0:n], preferred_element_type=F32) + jnp.dot(
                 act[0, :, fr : fr + n], wb[1, fr : fr + n], preferred_element_type=F32
             )
-            for c in first:
+            for c in out:
                 c.wait()
 
             @pl.when(i < 3)
@@ -638,26 +674,25 @@
                 for c in h_in(i + 1):
                     c.start()
 
-            pl.when(i == 0)(lambda: arrive(1))
-            u = jnp.dot(act[1, :, 0:d], wb[0, d : 2 * d], preferred_element_type=F32)
-            hout[0, 0:sub] = jax.nn.gelu(u, approximate=True).astype(BF16)
+            pl.when(i == 0)(lambda: arrive(final))
+            hout[0, 0:sub, 0 : 2 * w] = hidden(final)
             pl.when(i < 3)(lambda: xn_in(i + 1).start())
-            second = []
+            out = []
             for q in range(2):
-                second.append(
+                out.append(
                     pltpu.make_async_copy(
-                        hout.at[0, 0:sub, q * cb : (q + 1) * cb], h_at(i, q, t0 + cb, cb), h_sem.at[1, q]
+                        hout.at[0, 0:sub, q * w : (q + 1) * w], h_at(i, q, t0 + off, w), h_sem.at[2, q]
                     )
                 )
-                second[-1].start()
-            pout[0] += jnp.dot(hout[0, 0:sub, 0:cb], wb[1, n:fr], preferred_element_type=F32) + jnp.dot(
-                hout[0, 0:sub, cb : 2 * cb], wb[1, fr + n : kr], preferred_element_type=F32
+                out[-1].start()
+            pout[0] += jnp.dot(hout[0, 0:sub, 0:w], wb[1, n:fr], preferred_element_type=F32) + jnp.dot(
+                hout[0, 0:sub, w : 2 * w], wb[1, fr + n : kr], preferred_element_type=F32
             )
-            out = p_out(psend, zero, i, 0)
-            out.start()
-            out.wait()
+            sent = p_out(psend, zero, i, 0)
+            sent.start()
+            sent.wait()
             p_x(i, 0).start()
-            for c in second:
+            for c in out:
                 c.wait()
             return carry
 
@@ -682,7 +717,7 @@
             w1_yr(j).wait_send()
             w1_f(j).wait_send()
 
-    for t in range(2):
+    for t in range(len(tail)):
         w1_yt(t).wait_send()
         w1_ft(t).wait_send()
 
@@ -760,14 +795,14 @@
                 pltpu.VMEM((2, 2 * fq, c2), BF16),
                 pltpu.VMEM((2, 2 * sub, c1), BF16),
                 pltpu.VMEM((2, sub, c2), F32),
-                pltpu.VMEM((sub, c2), F32),
+                pltpu.VMEM((2, sub, c2), F32),
                 pltpu.VMEM((2, sub, c2), F32),
                 pltpu.VMEM((2, sub, c2), BF16),
-                pltpu.VMEM((2, sub, c2), BF16),
+                pltpu.VMEM((sub, c2), BF16),
                 pltpu.VMEM((1, d), F32),
-                dma((2, 2)), dma((2, 4)), dma((2, 2)), dma((3,)), dma((4,)), dma((2, 2)), dma((2, 2, 2)),
+                dma((2, 2)), dma((2, 4)), dma((3, 2)), dma((3,)), dma((3,)), dma((2, 3)), dma((3, 2, 2)),
                 dma((NX,)), dma((NX,)), dma((2,)), dma((2,)),
-                dma((N1 + 2,)), dma((N1 + 2,)), dma((N1 + 1,)), dma((N1 + 1,)), dma((N1 + 2,)), dma((N1 + 2,)),
+                dma((N1 + 3,)), dma((N1 + 3,)), dma((N1 + 1,)), dma((N1 + 1,)), dma((N1 + 3,)), dma((N1 + 3,)),
                 dma((N2 + 4,)), dma((N2 + 4,)), dma((N2 + 1,)), dma((N2 + 1,)), dma((N2 + 2,)), dma((N2 + 2,)),
                 dma((8 * N2,)), dma((8 * N2,)),
             ],

time: 1890 us -> 1860 us (0.984)
  Pallas kernels: 1890 us -> 1860 us
    pallas_call x1, Pallas kernels: 1870 us -> 1840 us  [body(): pl.pallas_call(_kernel, name='mlp', out_shape=outs, in_specs=[pl.BlockSpe...]
where the time goes in v4:
time: 1860 us
  Pallas kernels  1860 us (100%)
    pallas_call x1, Pallas kernels, body(): pl.pallas_call(_kernel, name='mlp', out_shape=outs, in_specs=[pl.BlockSpe...  1840 us

profile of v4, /device:TPU:0, one launch (start us, length us, event | category | flops | bytes accessed | tf_op | source)
XLA Modules:
  0.0 1859.8 jit_solution(4944628163994626568)
XLA Ops:
  0.0 1842.5 %mlp.1 = (bf16[2048,6144]{1,0:T(8,128)(2,1)}, bf16[4096,6144]{1,0:T(8,128)(2,1)}, bf16[3072,512]{1,0:T(8,128)(2,1)}, bf16[3072,6656]{1,0:T(8,128)(2,1)}, bf16[30...) custom-call(bf16[2048,6144]{1,0:T(8,128)(2,1)} %x.1, ...), custom_call_target="tpu_custom_call" | custom-call | tf_op jit(solution)/shard_map/mlp/pallas_call | solution.py:787
  1842.5 17.3 put.1

commit v5 on v4

--- a/solution.py
+++ b/solution.py
@@ -14,6 +14,7 @@
 NR = N1 - 1
 N2 = 6
 NX = 8
+BOTH = range(2)
 AHEAD = 3
 
 STEPS1 = (
@@ -35,8 +36,8 @@
 LAST = 2 * N2 - 1
 R, A, B = ((lambda k, t=t: (t, k)) for t in (REM, OWN, END))
 VISITS = (
-    R(1), R(2), R(3), R(4),
-    R(5), A(0), A(1), R(6), A(2), B(0), B(1), A(3), R(7), B(2), A(4), A(5), R(8), B(3), A(6), A(7), B(4), B(5),
+    *map(R, range(1, 6)),
+    A(0), A(1), R(6), A(2), B(0), B(1), A(3), R(7), B(2), A(4), A(5), R(8), B(3), A(6), A(7), B(4), B(5),
     R(9), A(8), B(6), A(9), B(7), R(10), B(8), A(10), R(11), A(11), B(9), B(10), B(11),
 )
 BREAK2 = 4
@@ -47,7 +48,8 @@
 
 
 def _tail(c1):
-    return ((0, c1 // 2), (c1 // 2, c1 // 2))
+    w = c1 // 2
+    return ((0, w), (w, w))
 
 
 def _where(cond, a, b):
@@ -87,7 +89,7 @@
 
 def _kernel(
     x, gamma, w1, w2,
-    y, xn, w1e, w1far, w1so, w1sf, w2e, w2far, w2so, w2sf, h, psend, pown, precv,
+    y, xlast, olast, xn, w1e, w1far, w1so, w1sf, w2e, w2far, w2so, w2sf, h, psend, pown, precv,
     act, wb, hout, pout, pin, pback, xin, yout, gam,
     act_sem, w_sem, h_sem, io_sem, out_sem, in_sem, tail_sem,
     xn_s, xn_r, e_s, e_r, w1y_s, w1y_r, w1c_s, w1c_r, w1f_s, w1f_r,
@@ -293,7 +295,7 @@
             c.start() if go else c.wait()
 
         if not go:
-            for i in range(2):
+            for i in BOTH:
                 load(i, w1far, cols1(j))
             return
         pl.when((q == 0) & (j < N1))(lambda: load(0, w1, cols1(j)))
@@ -482,7 +484,7 @@
                 todo.append(lambda k=k: w2_c(k).wait_recv() if k < N2 else w2_ff(k - N2).wait_recv())
             if n == min(at[B(k)] for k in range(N2)):
                 todo.append(lambda: w2_ce().wait_recv())
-            for g in range(2):
+            for g in BOTH:
                 if n == min(at[B(N2 + 3 * g + k)] for k in range(3)):
                     todo.append(lambda g=g: w2_fg(g).wait_recv())
             if todo:
@@ -499,16 +501,21 @@
         ycol = pl.multiple_of(_where(k < N2, near, away) + (k % N2) * c2, c2)
         return pltpu.make_async_copy(yout, y.at[hrows(i), pl.ds(ycol, c2)], out_sem.at[2])
 
+    def last_out(to, slot):
+        return pltpu.make_async_copy(pout.at[slot], to, out_sem.at[slot])
+
     def finish(typ, k, i, slot):
-        @pl.when((typ == REM) | (typ == OWN))
+        outside = (k == LAST) & (i == 3)
+
+        @pl.when((typ == REM) | (typ == OWN) | ((typ == END) & outside))
         def _():
             p_out(pown, k, i, slot).wait()
 
-        @pl.when(typ == REM)
+        @pl.when((typ == REM) & jnp.logical_not(outside))
         def _():
             p_x(i, k).start()
 
-        @pl.when(typ == END)
+        @pl.when((typ == END) & jnp.logical_not(outside))
         def _():
             y_out(k, i).wait()
 
@@ -551,9 +558,17 @@
 
                 finish(btyp, bk, bi, 1 - slot)
                 pl.when(typ == OWN)(lambda: p_out(pown, k, i, slot).start())
-                pl.when(typ == REM)(lambda: p_out(psend, k, i, slot).start())
-
-                @pl.when(typ == END)
+                outside = (k == LAST) & last
+                inside = jnp.logical_not(outside)
+                pl.when((typ == REM) & inside)(lambda: p_out(psend, k, i, slot).start())
+                pl.when((typ == REM) & outside)(lambda: last_out(xlast, slot).start())
+
+                @pl.when((typ == END) & outside)
+                def _():
+                    pout[slot] = pback[slot] + pout[slot]
+                    last_out(olast, slot).start()
+
+                @pl.when((typ == END) & inside)
                 def _():
                     @pl.when(k == LAST)
                     def _():
@@ -590,7 +605,7 @@
                     wb.at[0, r + part * half : r + (part + 1) * half, at + q * w : at + (q + 1) * w],
                     tail_sem.at[t, part, q],
                 )
-                for q in range(2)
+                for q in BOTH
             ]
 
         def xn_in(i):
@@ -602,17 +617,21 @@
         def h_in(i):
             return [
                 pltpu.make_async_copy(h_at(i, q, 0, t0), act.at[0, :, q * fr : q * fr + t0], act_sem.at[0, q])
-                for q in range(2)
+                for q in BOTH
             ]
 
-        def hidden(t):
+        def first_sum(block):
+            return remote(pout.at[0, block], precv.at[block, 0:c2], p_s.at[0], p_r.at[0], to_x)
+
+        def hidden(t, block=everything):
             r, at = lanes(t)
-            u = jnp.dot(act[1, :, 0:d], wb[0, r : r + d, at : at + 2 * tail[t][1]], preferred_element_type=F32)
+            u = jnp.dot(act[1, block, 0:d], wb[0, r : r + d, at : at + 2 * tail[t][1]], preferred_element_type=F32)
             return jax.nn.gelu(u, approximate=True).astype(BF16)
 
         def arrive(t):
             w1_yt(t).wait_recv()
             w1_ft(t).start()
+            w_tail(t, 1)[0].start()
             if t == final:
                 w1_y(N1 - 1).start()
                 w1_e().wait_recv()
@@ -621,12 +640,11 @@
                 w2_yf(1).start()
                 w2_e().wait_recv()
             w1_ft(t).wait_recv()
-            for c in w_tail(t, 1):
-                c.start()
+            w_tail(t, 1)[1].start()
             if t == final:
                 w1_ce().start()
                 w2_ce().start()
-            for part in range(2):
+            for part in BOTH:
                 for c in w_tail(t, part):
                     c.wait()
 
@@ -654,7 +672,7 @@
                     for c in h_in(i):
                         c.wait()
                 off, w = tail[t]
-                for q in range(2):
+                for q in BOTH:
                     at = q * fr + t0 + off
                     act[0, :, at : at + w] = g[:, q * w : (q + 1) * w]
                     out.append(
@@ -663,7 +681,8 @@
                     out[-1].start()
             off, w = tail[final]
             n = fr - w
-            pout[0] = jnp.dot(act[0, :, 0:n], wb[1, 0:n], preferred_element_type=F32) + jnp.dot(
+            slot = _where(i == 0, 0, 1)
+            pout[slot] = jnp.dot(act[0, :, 0:n], wb[1, 0:n], preferred_element_type=F32) + jnp.dot(
                 act[0, :, fr : fr + n], wb[1, fr : fr + n], preferred_element_type=F32
             )
             for c in out:
@@ -675,28 +694,41 @@
                     c.start()
 
             pl.when(i == 0)(lambda: arrive(final))
-            hout[0, 0:sub, 0 : 2 * w] = hidden(final)
+            block = sub // 2
+
+            @pl.loop(0, 2)
+            def _(m):
+                at = pl.ds(pl.multiple_of(m * block, block), block)
+                g = hidden(final, at)
+                hout[0, at, 0 : 2 * w] = g
+                pout[slot, at] += jnp.dot(g[:, 0:w], wb[1, n:fr], preferred_element_type=F32) + jnp.dot(
+                    g[:, w : 2 * w], wb[1, fr + n : kr], preferred_element_type=F32
+                )
+                pl.when(i == 0)(lambda: first_sum(at).start())
+
             pl.when(i < 3)(lambda: xn_in(i + 1).start())
             out = []
-            for q in range(2):
+            for q in BOTH:
                 out.append(
                     pltpu.make_async_copy(
                         hout.at[0, 0:sub, q * w : (q + 1) * w], h_at(i, q, t0 + off, w), h_sem.at[2, q]
                     )
                 )
                 out[-1].start()
-            pout[0] += jnp.dot(hout[0, 0:sub, 0:w], wb[1, n:fr], preferred_element_type=F32) + jnp.dot(
-                hout[0, 0:sub, w : 2 * w], wb[1, fr + n : kr], preferred_element_type=F32
-            )
-            sent = p_out(psend, zero, i, 0)
-            sent.start()
-            sent.wait()
-            p_x(i, 0).start()
+
+            @pl.when(i > 0)
+            def _():
+                sent = p_out(psend, zero, i, 1)
+                sent.start()
+                sent.wait()
+                p_x(i, 0).start()
+
             for c in out:
                 c.wait()
             return carry
 
         lax.fori_loop(0, 4, tile_, jnp.int32(0))
+        p_x(0, 0).wait_send()
 
     @pl.loop(0, 2)
     def _(phase):
@@ -730,7 +762,7 @@
     w1_e().wait_send()
     w2_e().wait_send()
     w2_ce().wait_send()
-    for g in range(2):
+    for g in BOTH:
         for c in w2_yg(g):
             c.wait_send()
         w2_fg(g).wait_send()
@@ -739,7 +771,7 @@
     def _(t):
         xn_x(t).wait_send()
 
-    @pl.loop(0, 2 * N2 * 4)
+    @pl.loop(1, 2 * N2 * 4 - 1)
     def _(s):
         p_x(s % 4, s // 4).wait_send()
 
@@ -778,12 +810,15 @@
         dma = pltpu.SemaphoreType.DMA
         outs = (
             hbm(rows, d),
+            hbm(sub, c2, dtype=F32),
+            hbm(sub, c2, dtype=F32),
             hbm(2 * rows, d),
             hbm(half, c1), hbm(half, fq + c1), hbm(half, fq + c1), hbm(half, fq + c1),
             hbm(c1, half), hbm(fq + c1, half), hbm(fq + c1, half), hbm(fq + c1, half),
             hbm(2 * rows, 2 * (fq + c1)),
             hbm(rows, d, dtype=F32), hbm(rows, d, dtype=F32), hbm(rows, d, dtype=F32),
         )
+        sent = (NX, 2, N1 + 3, N1 + 1, N1 + 3, N2 + 4, N2 + 1, N2 + 2, 8 * N2)
         out = pl.pallas_call(
             _kernel,
             name="mlp",
@@ -800,17 +835,15 @@
                 pltpu.VMEM((2, sub, c2), BF16),
                 pltpu.VMEM((sub, c2), BF16),
                 pltpu.VMEM((1, d), F32),
-                dma((2, 2)), dma((2, 4)), dma((3, 2)), dma((3,)), dma((3,)), dma((2, 3)), dma((3, 2, 2)),
-                dma((NX,)), dma((NX,)), dma((2,)), dma((2,)),
-                dma((N1 + 3,)), dma((N1 + 3,)), dma((N1 + 1,)), dma((N1 + 1,)), dma((N1 + 3,)), dma((N1 + 3,)),
-                dma((N2 + 4,)), dma((N2 + 4,)), dma((N2 + 1,)), dma((N2 + 1,)), dma((N2 + 2,)), dma((N2 + 2,)),
-                dma((8 * N2,)), dma((8 * N2,)),
+                *(dma(n) for n in ((2, 2), (2, 4), (3, 2), (3,), (3,), (2, 3), (2, 2, 2))),
+                *(dma((n,)) for n in sent for _ in BOTH),
             ],
             compiler_params=pltpu.CompilerParams(
                 collective_id=0, has_side_effects=True, vmem_limit_bytes=67_000_000
             ),
         )(x, gamma.reshape(1, d), w1, w2)
-        return pl.pallas_call(
+        got = lax.ppermute(out[1], "tp", [(i, (i + 2) % 4) for i in range(4)])
+        y = pl.pallas_call(
             _put,
             name="put",
             out_shape=hbm(rows, d),
@@ -818,7 +851,11 @@
             out_specs=pl.BlockSpec(memory_space=pl.ANY),
             scratch_shapes=[pltpu.VMEM((PUTS, rows // PUTS, d), BF16), dma((PUTS,)), dma((PUTS,))],
             compiler_params=pltpu.CompilerParams(vmem_limit_bytes=40_000_000),
+            cost_estimate=pl.CostEstimate(flops=30_000_000_000, bytes_accessed=4 * rows * d, transcendentals=0),
         )(out[0])
+        at = (3 * sub, (1 - lax.axis_index("fsdp")) * half + (N2 - 1) * c2)
+        tile = lax.dynamic_slice(x, at, (sub, c2)).astype(F32) + (out[2] + got)
+        return lax.dynamic_update_slice(y, tile.astype(BF16), at)
 
     return jax.shard_map(
         body,

time: 1860 us -> 1850 us (level)
  Pallas kernels: 1860 us -> 1840 us
    pallas_call x1, Pallas kernels: 1840 us -> 1820 us  [body(): pl.pallas_call(_kernel, name='mlp', out_shape=outs, in_specs=[pl.BlockSpe...]
  transfers between devices with their start and end apart: 0 -> 1, of which waited for: 0 -> 1; matrix products, arithmetic and copies ran while one was open for 0% -> 0% of each run, Pallas kernels for 0% -> 1%
where the time goes in v5:
time: 1850 us
  Pallas kernels  1840 us (99%)
    pallas_call x1, Pallas kernels, body(): pl.pallas_call(_kernel, name='mlp', out_shape=outs, in_specs=[pl.BlockSpe...  1820 us
  transfers between devices with their start and end apart: 1, of which 1 were waited for; matrix products, arithmetic and copies ran while one was open for 0% of the time, Pallas kernels for 1%

profile of v5, /device:TPU:0, one launch (start us, length us, event | category | flops | bytes accessed | tf_op | source)
XLA Modules:
  0.0 1848.5 jit_solution(18437413378587687449)
XLA Ops:
  0.0 1822.7 %mlp.1 = (bf16[2048,6144]{1,0:T(8,128)(2,1)}, f32[512,512]{1,0:T(8,128)}, f32[512,512]{1,0:T(8,128)}, bf16[4096,6144]{1,0:T(8,128)(2,1)}, bf16[3072,512]{1,0:T(8...) custom-call(bf16[2048,6144]{1,0:T(8,128)(2,1)} %x.1, ...), custom_call_target="tpu_custom_call" | custom-call | tf_op jit(solution)/shard_map/mlp/pallas_call | solution.py:822
  1822.7 1.5 collective-permute-start
  1824.2 0.0 copy-start
  1824.2 17.4 put.1
  1841.6 4.8 collective-permute-done
  1846.4 0.0 copy-done
  1846.4 2.1 fusion
Async XLA Ops:
  1822.7 23.7 %collective-permute-start = (f32[512,512]{1,0:T(8,128)}, f32[512,512]{1,0:T(8,128)S(1)}, u32[]{:S(2)}, u32[]{:S(2)}) collective-permute-start(f32[512,512]{1,0:T(8,128)} %get-tuple-element.10), channel_id=1, source_target_pairs={{0,2},{1,3},{2,0},{3,1},{4,6},{5,7},{6,4},{7,5}} | collective-permute-start | bytes 3145736 | tf_op jit(solution)/shard_map/ppermute | solution.py:845
  1824.2 22.2 %copy-start = (f32[512,512]{1,0:T(8,128)S(1)}, f32[512,512]{1,0:T(8,128)}, u32[]{:S(2)}) copy-start(f32[512,512]{1,0:T(8,128)} %get-tuple-element.9) | copy-start | bytes 3145732

commit v6 on v5

--- a/solution.py
+++ b/solution.py
@@ -42,9 +42,10 @@
 )
 BREAK2 = 4
 PASS_F = {A(1): 0, B(1): 1, A(5): 2, B(5): 3, B(7): 4, R(11): 5}
-PASS_G = {B(4): 0, A(11): 1}
+PASS_G = {B(4): 0, A(11): 1, B(9): 2, B(10): 3}
 SEND_F = {R(2): (2,), R(5): (3, 4), R(7): (5,)}
-SEND_G = {R(2): 0, R(7): 1}
+SEND_G = {R(2): (0,), R(7): (1, 2, 3)}
+PARTS_G = ((0, 3), (3, 1), (4, 1), (5, 1))
 
 
 def _tail(c1):
@@ -110,7 +111,6 @@
     t0 = fr - c1
     kr = 2 * fr
     ke = 4 * c1
-    wide = half // 2
     piece = rows // NX
     near = pl.multiple_of(a * half, half)
     away = pl.multiple_of((1 - a) * half, half)
@@ -170,14 +170,15 @@
         at = (pl.ds(0, fr), cols2(k))
         return remote(w2.at[at], w2far.at[at], w2y_s.at[k], w2y_r.at[k], to_y)
 
+    def cols_g(g):
+        k, n = PARTS_G[g]
+        return pl.ds(k * c2, n * c2)
+
     def w2_yg(g):
-        at = (pl.ds(fr, c1), pl.ds(g * wide, wide))
-        to = (pl.ds(fq, c1), pl.ds(g * wide, wide))
+        at, to, n = (pl.ds(fr, c1), cols_g(g)), (pl.ds(fq, c1), cols_g(g)), N2 + g + g
         return (
-            remote(w2.at[at], w2far.at[at], w2y_s.at[N2 + 2 * g], w2y_r.at[N2 + 2 * g], to_y),
-            remote(
-                w2e.at[:, pl.ds(g * wide, wide)], w2far.at[to], w2y_s.at[N2 + 2 * g + 1], w2y_r.at[N2 + 2 * g + 1], to_y
-            ),
+            remote(w2.at[at], w2far.at[at], w2y_s.at[n], w2y_r.at[n], to_y),
+            remote(w2e.at[:, cols_g(g)], w2far.at[to], w2y_s.at[n + 1], w2y_r.at[n + 1], to_y),
         )
 
     def w2_c(k):
@@ -192,7 +193,7 @@
         return remote(w2far.at[at], w2sf.at[at], w2f_s.at[k], w2f_r.at[k], to_c)
 
     def w2_fg(g):
-        at = (pl.ds(fr, 2 * c1), pl.ds(g * wide, wide))
+        at = (pl.ds(fr, 2 * c1), cols_g(g))
         return remote(w2far.at[at], w2sf.at[at], w2f_s.at[N2 + g], w2f_r.at[N2 + g], to_c)
 
     def xrows(t):
@@ -227,7 +228,7 @@
         return [
             pltpu.make_async_copy(
                 x.at[xrows(t), pl.ds(off, half)],
-                act.at[slot, 0:piece, i * half : (i + 1) * half],
+                act.at[slot, :piece, i * half : (i + 1) * half],
                 act_sem.at[slot, i],
             )
             for i, off in enumerate((near, away))
@@ -255,12 +256,12 @@
         @pl.loop(0, piece // 16)
         def _(r):
             at = pl.multiple_of(r * 16, 16)
-            xs = act[slot, pl.ds(at, 16), 0:d].astype(F32)
+            xs = act[slot, pl.ds(at, 16), :d].astype(F32)
             xc = xs - jnp.mean(xs, axis=1, keepdims=True)
             var = jnp.mean(xc * xc, axis=1, keepdims=True)
-            act[slot, pl.ds(piece + at, 16), 0:d] = (xc * lax.rsqrt(var + EPS) * gam[...]).astype(BF16)
-
-        out = pltpu.make_async_copy(act.at[slot, piece : 2 * piece, 0:d], xn.at[xrows(t)], io_sem.at[2])
+            act[slot, pl.ds(piece + at, 16), :d] = (xc * lax.rsqrt(var + EPS) * gam[...]).astype(BF16)
+
+        out = pltpu.make_async_copy(act.at[slot, piece : 2 * piece, :d], xn.at[xrows(t)], io_sem.at[2])
         out.start()
         out.wait()
 
@@ -396,7 +397,7 @@
             @pl.loop(0, _where(two, 2, 1))
             def _(i):
                 u = jnp.dot(
-                    act[aslot, :, pl.ds(pl.multiple_of(i * d, d), d)], wb[wslot, 0:d], preferred_element_type=F32
+                    act[aslot, :, pl.ds(pl.multiple_of(i * d, d), d)], wb[wslot, :d], preferred_element_type=F32
                 )
                 hout[s % 2, pl.ds(pl.multiple_of(i * sub, sub), sub)] = jax.nn.gelu(u, approximate=True).astype(BF16)
                 h_out(s, i).start()
@@ -419,12 +420,12 @@
 
         @pl.when(typ != END)
         def _():
-            wait_or_start(pltpu.make_async_copy(h.at[hrows(r), 0:kr], act.at[slot, :, 0:kr], act_sem.at[slot, 0]))
+            wait_or_start(pltpu.make_async_copy(h.at[hrows(r), :kr], act.at[slot, :, :kr], act_sem.at[slot, 0]))
 
         @pl.when(typ == END)
         def _():
             wait_or_start(
-                pltpu.make_async_copy(h.at[hrows(r), kr : kr + ke], act.at[slot, :, 0:ke], act_sem.at[slot, 0])
+                pltpu.make_async_copy(h.at[hrows(r), kr : kr + ke], act.at[slot, :, :ke], act_sem.at[slot, 0])
             )
             ycol = pl.multiple_of(_where(k < N2, near, away) + (k % N2) * c2, c2)
             wait_or_start(pltpu.make_async_copy(pown.at[hrows(i), cols2(k)], pback.at[slot], in_sem.at[slot, 0]))
@@ -471,8 +472,8 @@
             todo = []
             for u in SEND_F.get(visit, ()):
                 todo.append(lambda u=u: w2_yf(u).start())
-            if visit in SEND_G:
-                todo.append(lambda g=SEND_G[visit]: [c.start() for c in w2_yg(g)])
+            for g in SEND_G.get(visit, ()):
+                todo.append(lambda g=g: [c.start() for c in w2_yg(g)])
             if visit in PASS_F:
                 u = PASS_F[visit]
                 todo.append(lambda u=u: (w2_yf(u).wait_recv(), w2_ff(u).start()))
@@ -484,8 +485,8 @@
                 todo.append(lambda k=k: w2_c(k).wait_recv() if k < N2 else w2_ff(k - N2).wait_recv())
             if n == min(at[B(k)] for k in range(N2)):
                 todo.append(lambda: w2_ce().wait_recv())
-            for g in BOTH:
-                if n == min(at[B(N2 + 3 * g + k)] for k in range(3)):
+            for g, (k0, nk) in enumerate(PARTS_G):
+                if n == min(at[B(N2 + k)] for k in range(k0, k0 + nk)):
                     todo.append(lambda g=g: w2_fg(g).wait_recv())
             if todo:
 
@@ -550,11 +551,11 @@
 
                 @pl.when(typ != END)
                 def _():
-                    pout[slot] = jnp.dot(act[slot, :, 0:kr], wb[wslot, 0:kr], preferred_element_type=F32)
+                    pout[slot] = jnp.dot(act[slot, :, :kr], wb[wslot, :kr], preferred_element_type=F32)
 
                 @pl.when(typ == END)
                 def _():
-                    pout[slot] = jnp.dot(act[slot, :, 0:ke], wb[wslot, 0:ke], preferred_element_type=F32)
+                    pout[slot] = jnp.dot(act[slot, :, :ke], wb[wslot, :ke], preferred_element_type=F32)
 
                 finish(btyp, bk, bi, 1 - slot)
                 pl.when(typ == OWN)(lambda: p_out(pown, k, i, slot).start())
@@ -609,7 +610,7 @@
             ]
 
         def xn_in(i):
-            return pltpu.make_async_copy(xn.at[hrows(4 + i)], act.at[1, :, 0:d], act_sem.at[1, 0])
+            return pltpu.make_async_copy(xn.at[hrows(4 + i)], act.at[1, :, :d], act_sem.at[1, 0])
 
         def h_at(i, q, col, width):
             return h.at[hrows(4 + i), q * fr + col : q * fr + col + width]
@@ -621,11 +622,11 @@
             ]
 
         def first_sum(block):
-            return remote(pout.at[0, block], precv.at[block, 0:c2], p_s.at[0], p_r.at[0], to_x)
+            return remote(pout.at[0, block], precv.at[block, :c2], p_s.at[0], p_r.at[0], to_x)
 
         def hidden(t, block=everything):
             r, at = lanes(t)
-            u = jnp.dot(act[1, block, 0:d], wb[0, r : r + d, at : at + 2 * tail[t][1]], preferred_element_type=F32)
+            u = jnp.dot(act[1, block, :d], wb[0, r : r + d, at : at + 2 * tail[t][1]], preferred_element_type=F32)
             return jax.nn.gelu(u, approximate=True).astype(BF16)
 
         def arrive(t):
@@ -682,7 +683,7 @@
             off, w = tail[final]
             n = fr - w
             slot = _where(i == 0, 0, 1)
-            pout[slot] = jnp.dot(act[0, :, 0:n], wb[1, 0:n], preferred_element_type=F32) + jnp.dot(
+            pout[slot] = jnp.dot(act[0, :, :n], wb[1, :n], preferred_element_type=F32) + jnp.dot(
                 act[0, :, fr : fr + n], wb[1, fr : fr + n], preferred_element_type=F32
             )
             for c in out:
@@ -700,8 +701,8 @@
             def _(m):
                 at = pl.ds(pl.multiple_of(m * block, block), block)
                 g = hidden(final, at)
-                hout[0, at, 0 : 2 * w] = g
-                pout[slot, at] += jnp.dot(g[:, 0:w], wb[1, n:fr], preferred_element_type=F32) + jnp.dot(
+                hout[0, at, :2 * w] = g
+                pout[slot, at] += jnp.dot(g[:, :w], wb[1, n:fr], preferred_element_type=F32) + jnp.dot(
                     g[:, w : 2 * w], wb[1, fr + n : kr], preferred_element_type=F32
                 )
                 pl.when(i == 0)(lambda: first_sum(at).start())
@@ -711,7 +712,7 @@
             for q in BOTH:
                 out.append(
                     pltpu.make_async_copy(
-                        hout.at[0, 0:sub, q * w : (q + 1) * w], h_at(i, q, t0 + off, w), h_sem.at[2, q]
+                        hout.at[0, :sub, q * w : (q + 1) * w], h_at(i, q, t0 + off, w), h_sem.at[2, q]
                     )
                 )
                 out[-1].start()
@@ -762,7 +763,7 @@
     w1_e().wait_send()
     w2_e().wait_send()
     w2_ce().wait_send()
-    for g in BOTH:
+    for g in range(len(PARTS_G)):
         for c in w2_yg(g):
             c.wait_send()
         w2_fg(g).wait_send()
@@ -818,7 +819,7 @@
             hbm(2 * rows, 2 * (fq + c1)),
             hbm(rows, d, dtype=F32), hbm(rows, d, dtype=F32), hbm(rows, d, dtype=F32),
         )
-        sent = (NX, 2, N1 + 3, N1 + 1, N1 + 3, N2 + 4, N2 + 1, N2 + 2, 8 * N2)
+        sent = (NX, 2, N1 + 3, N1 + 1, N1 + 3, 3 * N2, N2 + 1, 2 * N2, 8 * N2)
         out = pl.pallas_call(
             _kernel,
             name="mlp",

time: 1850 us -> 1850 us (level)
  no operation moved by 1% of the time
where the time goes in v6:
time: 1850 us
  Pallas kernels  1840 us (99%)
    pallas_call x1, Pallas kernels, body(): pl.pallas_call(_kernel, name='mlp', out_shape=outs, in_specs=[pl.BlockSpe...  1820 us
  transfers between devices with their start and end apart: 1, of which 1 were waited for; matrix products, arithmetic and copies ran while one was open for 0% of the time, Pallas kernels for 1%

profile of v6, /device:TPU:0, one launch (start us, length us, event | category | flops | bytes accessed | tf_op | source)
XLA Modules:
  0.0 1845.9 jit_solution(5153085789056481733)
XLA Ops:
  0.0 1818.5 %mlp.1 = (bf16[2048,6144]{1,0:T(8,128)(2,1)}, f32[512,512]{1,0:T(8,128)}, f32[512,512]{1,0:T(8,128)}, bf16[4096,6144]{1,0:T(8,128)(2,1)}, bf16[3072,512]{1,0:T(8...) custom-call(bf16[2048,6144]{1,0:T(8,128)(2,1)} %x.1, ...), custom_call_target="tpu_custom_call" | custom-call | tf_op jit(solution)/shard_map/mlp/pallas_call | solution.py:823
  1818.5 0.3 collective-permute-start
  1818.7 0.0 copy-start
  1818.7 17.4 put.1
  1836.1 7.7 collective-permute-done
  1843.8 0.0 copy-done
  1843.8 2.1 fusion
Async XLA Ops:
  1818.5 25.3 %collective-permute-start = (f32[512,512]{1,0:T(8,128)}, f32[512,512]{1,0:T(8,128)S(1)}, u32[]{:S(2)}, u32[]{:S(2)}) collective-permute-start(f32[512,512]{1,0:T(8,128)} %get-tuple-element.10), channel_id=1, source_target_pairs={{0,2},{1,3},{2,0},{3,1},{4,6},{5,7},{6,4},{7,5}} | collective-permute-start | bytes 3145736 | tf_op jit(solution)/shard_map/ppermute | solution.py:846
  1818.7 25.1 %copy-start = (f32[512,512]{1,0:T(8,128)S(1)}, f32[512,512]{1,0:T(8,128)}, u32[]{:S(2)}) copy-start(f32[512,512]{1,0:T(8,128)} %get-tuple-element.9) | copy-start | bytes 3145732

commit v7 on v6

--- a/solution.py
+++ b/solution.py
@@ -12,6 +12,7 @@
 
 N1 = 12
 NR = N1 - 1
+NT = NR - 1
 N2 = 6
 NX = 8
 BOTH = range(2)
@@ -28,7 +29,7 @@
     ((7, 1), (4, 1)),
     ((0, 8), (5, 1)),
     ((8, 2), (2, 2)),
-    ((7, 6), (0, 2)),
+    ((7, 7), (0, 2)),
 )
 BREAK1 = 10
 
@@ -50,7 +51,7 @@
 
 def _tail(c1):
     w = c1 // 2
-    return ((0, w), (w, w))
+    return ((0, w), (w, w // 2))
 
 
 def _where(cond, a, b):
@@ -78,7 +79,7 @@
 
 
 def _first_tile(j):
-    return _where(j < 7, 0, _where(j < NR - 1, 2, _where(j == NR - 1, 9, 0)))
+    return _where((j >= 7) & (j < NT), 2, 0)
 
 
 def _visit(v):
@@ -107,10 +108,11 @@
     c1 = fq // N1
     c2 = half // N2
     tail = _tail(c1)
-    fr = NR * c1
-    t0 = fr - c1
+    t0 = NT * c1
+    fr = t0 + sum(w for _, w in tail)
+    ce = fq - fr
     kr = 2 * fr
-    ke = 4 * c1
+    ke = 4 * ce
     piece = rows // NX
     near = pl.multiple_of(a * half, half)
     away = pl.multiple_of((1 - a) * half, half)
@@ -127,32 +129,38 @@
     def cols2(k):
         return pl.ds(pl.multiple_of(k * c2, c2), c2)
 
+    own_e = (everything, pl.ds(fr, ce))
+    ext_e = (everything, pl.ds(fq, ce))
+
     def w1_y(j):
         return remote(w1.at[cols1(j)], w1far.at[cols1(j)], w1y_s.at[j], w1y_r.at[j], to_y)
 
+    def w1_yo():
+        return remote(w1.at[own_e], w1far.at[own_e], w1y_s.at[NR], w1y_r.at[NR], to_y)
+
     def w1_ye():
-        return remote(w1e, w1far.at[cols1(N1)], w1y_s.at[N1], w1y_r.at[N1], to_y)
-
-    def w1_yr(j):
-        return remote(w1far.at[cols1(j)], w1far.at[cols1(j)], w1y_s.at[j], w1y_r.at[j], to_y)
+        return remote(w1e.at[:, :ce], w1far.at[ext_e], w1y_s.at[N1], w1y_r.at[N1], to_y)
 
     def w1_c(j):
         return remote(w1.at[cols1(j)], w1so.at[cols1(j)], w1c_s.at[j], w1c_r.at[j], to_c)
 
     def w1_ce():
-        return remote(w1e, w1so.at[cols1(N1)], w1c_s.at[N1], w1c_r.at[N1], to_c)
-
-    def w1_cr(j):
-        return remote(w1so.at[cols1(j)], w1so.at[cols1(j)], w1c_s.at[j], w1c_r.at[j], to_c)
+        return remote(w1e.at[:, :ce], w1so.at[ext_e], w1c_s.at[N1], w1c_r.at[N1], to_c)
 
     def w1_f(j):
         return remote(w1far.at[cols1(j)], w1sf.at[cols1(j)], w1f_s.at[j], w1f_r.at[j], to_c)
 
+    def w1_fo():
+        return remote(w1far.at[own_e], w1sf.at[own_e], w1f_s.at[NR], w1f_r.at[NR], to_c)
+
+    def w1_fe():
+        return remote(w1far.at[ext_e], w1sf.at[ext_e], w1f_s.at[N1], w1f_r.at[N1], to_c)
+
     def cols_t(t):
         return (everything, pl.ds(t0 + tail[t][0], tail[t][1]))
 
     def tail_at(t):
-        return NR - 1 if t == 0 else N1 + t
+        return NT if t == 0 else N1 + t
 
     def w1_yt(t):
         return remote(w1.at[cols_t(t)], w1far.at[cols_t(t)], w1y_s.at[tail_at(t)], w1y_r.at[tail_at(t)], to_y)
@@ -161,7 +169,7 @@
         return remote(w1far.at[cols_t(t)], w1sf.at[cols_t(t)], w1f_s.at[tail_at(t)], w1f_r.at[tail_at(t)], to_c)
 
     def w1_e():
-        return remote(w1.at[cols1(N1 - 1)], w1e, e_s.at[0], e_r.at[0], to_x)
+        return remote(w1.at[own_e], w1e.at[:, :ce], e_s.at[0], e_r.at[0], to_x)
 
     def w2_e():
         return remote(w2.at[fr:fq], w2e, e_s.at[1], e_r.at[1], to_x)
@@ -175,7 +183,7 @@
         return pl.ds(k * c2, n * c2)
 
     def w2_yg(g):
-        at, to, n = (pl.ds(fr, c1), cols_g(g)), (pl.ds(fq, c1), cols_g(g)), N2 + g + g
+        at, to, n = (pl.ds(fr, ce), cols_g(g)), (pl.ds(fq, ce), cols_g(g)), N2 + g + g
         return (
             remote(w2.at[at], w2far.at[at], w2y_s.at[n], w2y_r.at[n], to_y),
             remote(w2e.at[:, cols_g(g)], w2far.at[to], w2y_s.at[n + 1], w2y_r.at[n + 1], to_y),
@@ -186,14 +194,14 @@
         return remote(w2.at[at], w2so.at[pl.ds(0, fq), cols2(k)], w2c_s.at[k], w2c_r.at[k], to_c)
 
     def w2_ce():
-        return remote(w2e, w2so.at[fq : fq + c1], w2c_s.at[N2], w2c_r.at[N2], to_c)
+        return remote(w2e, w2so.at[fq : fq + ce], w2c_s.at[N2], w2c_r.at[N2], to_c)
 
     def w2_ff(k):
         at = (pl.ds(0, fr), cols2(k))
         return remote(w2far.at[at], w2sf.at[at], w2f_s.at[k], w2f_r.at[k], to_c)
 
     def w2_fg(g):
-        at = (pl.ds(fr, 2 * c1), cols_g(g))
+        at = (pl.ds(fr, 2 * ce), cols_g(g))
         return remote(w2far.at[at], w2sf.at[at], w2f_s.at[N2 + g], w2f_r.at[N2 + g], to_c)
 
     def xrows(t):
@@ -269,9 +277,6 @@
         def _():
             xn_x(t).start()
 
-    def hcol(j, q):
-        return pl.multiple_of(_where(j < NR, q * fr + j * c1, kr + (j - NR) * 2 * c1 + q * c1), c1)
-
     def tile_rows(m):
         return _where(m < 4, 2 * m, 2 + m), m < 4
 
@@ -300,7 +305,7 @@
                 load(i, w1far, cols1(j))
             return
         pl.when((q == 0) & (j < N1))(lambda: load(0, w1, cols1(j)))
-        pl.when((q == 0) & (j == N1))(lambda: load(0, w1e, (everything, everything)))
+        pl.when((q == 0) & (j >= N1))(lambda: load(0, w1e, cols1(j - N1)))
         pl.when(q == 0)(lambda: load(1, w1far, cols1(j)))
 
         @pl.when(q == 1)
@@ -315,18 +320,29 @@
 
     def arrive1(s):
         j, q, m = _step1(s)
-        first = m == _first_tile(j)
+        first = (m == _first_tile(j)) & (j < NT)
+
+        @pl.when((m == 0) & (q == 0))
+        def _():
+            pl.when(j == NT)(lambda: (w1_yo().wait_recv(), w1_fo().start()) and None)
+            pl.when(j == N1)(lambda: (w1_ye().wait_recv(), w1_fe().start()) and None)
+
+        @pl.when((m == 0) & (q == 1))
+        def _():
+            pl.when(j == NT)(lambda: w1_fo().wait_recv())
+            pl.when(j == NR)(lambda: w1_c(j).wait_recv())
+            pl.when(j == N1)(lambda: (w1_ce().wait_recv(), w1_fe().wait_recv()) and None)
 
         @pl.when(first & (q == 0))
         def _():
-            w1_yr(j).wait_recv()
+            w1_y(j).wait_recv()
             w1_f(j).start()
 
-            @pl.when(j + AHEAD < NR - 1)
+            @pl.when(j + AHEAD < NT)
             def _():
                 w1_y(j + AHEAD).start()
 
-            @pl.when(j + AHEAD == NR - 1)
+            @pl.when(j + AHEAD == NT)
             def _():
                 for t in range(len(tail)):
                     w1_yt(t).start()
@@ -345,7 +361,7 @@
 
         @pl.when(first & (q == 1))
         def _():
-            w1_cr(j).wait_recv()
+            w1_c(j).wait_recv()
             w1_f(j).wait_recv()
 
         for at, lo, hi in ((first2, 0, 4), (first3, 4, 6), (first4, 6, 8)):
@@ -360,19 +376,36 @@
         pl.when(a_new)(lambda: a1_in(m, aslot, True))
         pl.when(w_new)(lambda: w1_in(j, q, wslot, True))
 
-    def h_out(s, i):
+    def h_out(s, i, go):
         j, q, m = _step1(s)
         r0, _ = tile_rows(m)
-        return pltpu.make_async_copy(
-            hout.at[s % 2, pl.ds(pl.multiple_of(i * sub, sub), sub)],
-            h.at[hrows(r0 + i), pl.ds(hcol(j, q), c1)],
-            h_sem.at[s % 2, i],
-        )
+        slot = s % 2
+        full = fr - t0
+
+        def part(at, w, col, sem):
+            c = pltpu.make_async_copy(
+                hout.at[slot, pl.ds(pl.multiple_of(i * sub, sub), sub), at : at + w],
+                h.at[hrows(r0 + i), pl.ds(pl.multiple_of(col, c1 - full), w)],
+                h_sem.at[sem, i],
+            )
+            c.start() if go else c.wait()
+
+        own, ext = kr + q * ce, kr + (2 + q) * ce
+        pl.when(j < NT)(lambda: part(0, c1, q * fr + j * c1, slot))
+
+        @pl.when(j == NT)
+        def _():
+            part(0, full, q * fr + t0, slot)
+            part(full, c1 - full, own, 2 + slot)
+
+        pl.when(j == NR)(lambda: part(0, c1, own + c1 - full, slot))
+        pl.when(j == N1)(lambda: part(0, c1, ext, slot))
+        pl.when(j > N1)(lambda: part(0, ce - c1, ext + c1, slot))
 
     def h_done(s):
         _, two = tile_rows(_step1(s)[2])
-        h_out(s, 0).wait()
-        pl.when(two)(lambda: h_out(s, 1).wait())
+        h_out(s, 0, False)
+        pl.when(two)(lambda: h_out(s, 1, False))
 
     def first_product(lo, hi):
         arrive1(lo)
@@ -400,7 +433,7 @@
                     act[aslot, :, pl.ds(pl.multiple_of(i * d, d), d)], wb[wslot, :d], preferred_element_type=F32
                 )
                 hout[s % 2, pl.ds(pl.multiple_of(i * sub, sub), sub)] = jax.nn.gelu(u, approximate=True).astype(BF16)
-                h_out(s, i).start()
+                h_out(s, i, True)
 
             return na, nw, _where(a_new, 1, 0), _where(w_new, 1, 0)
 
@@ -449,10 +482,8 @@
             load(1, fr, fr, sib, 0, kk)
 
         def rest(own, ext, ext_at, sib, kk):
-            load(0, 0, c1, own, fr, kk)
-            load(1, c1, c1, sib, fr, kk)
-            load(2, 2 * c1, c1, ext, ext_at, kk)
-            load(3, 3 * c1, c1, sib, fq, kk)
+            for n, (ref, from_) in enumerate(((own, fr), (sib, fr), (ext, ext_at), (sib, fq))):
+                load(n, n * ce, ce, ref, from_, kk)
 
         def both(side, kk, own, ext, ext_at, sib):
             pl.when(side & (typ != END))(lambda: main(own, sib, kk))
@@ -506,13 +537,13 @@
         return pltpu.make_async_copy(pout.at[slot], to, out_sem.at[slot])
 
     def finish(typ, k, i, slot):
-        outside = (k == LAST) & (i == 3)
+        outside = (k == LAST) & (i >= 2)
 
         @pl.when((typ == REM) | (typ == OWN) | ((typ == END) & outside))
         def _():
             p_out(pown, k, i, slot).wait()
 
-        @pl.when((typ == REM) & jnp.logical_not(outside))
+        @pl.when((typ == REM) & ((k < LAST) | (i < 3)))
         def _():
             p_x(i, k).start()
 
@@ -559,15 +590,16 @@
 
                 finish(btyp, bk, bi, 1 - slot)
                 pl.when(typ == OWN)(lambda: p_out(pown, k, i, slot).start())
-                outside = (k == LAST) & last
+                outside = (k == LAST) & (i >= 2)
                 inside = jnp.logical_not(outside)
-                pl.when((typ == REM) & inside)(lambda: p_out(psend, k, i, slot).start())
-                pl.when((typ == REM) & outside)(lambda: last_out(xlast, slot).start())
+                final = (k == LAST) & last
+                pl.when((typ == REM) & jnp.logical_not(final))(lambda: p_out(psend, k, i, slot).start())
+                pl.when((typ == REM) & final)(lambda: last_out(xlast, slot).start())
 
                 @pl.when((typ == END) & outside)
                 def _():
                     pout[slot] = pback[slot] + pout[slot]
-                    last_out(olast, slot).start()
+                    last_out(olast.at[pl.ds(pl.multiple_of((i - 2) * sub, sub), sub)], slot).start()
 
                 @pl.when((typ == END) & inside)
                 def _():
@@ -629,12 +661,13 @@
             u = jnp.dot(act[1, block, :d], wb[0, r : r + d, at : at + 2 * tail[t][1]], preferred_element_type=F32)
             return jax.nn.gelu(u, approximate=True).astype(BF16)
 
-        def arrive(t):
+        def arrive(t, meanwhile=lambda: None):
             w1_yt(t).wait_recv()
             w1_ft(t).start()
             w_tail(t, 1)[0].start()
+            meanwhile()
             if t == final:
-                w1_y(N1 - 1).start()
+                w1_yo().start()
                 w1_e().wait_recv()
                 w1_ye().start()
                 w2_yf(0).start()
@@ -649,18 +682,20 @@
                 for c in w_tail(t, part):
                     c.wait()
 
-        w1_c(NR - 1).wait_recv()
+        w1_c(NT).wait_recv()
         for t in range(len(tail)):
             for c in w_tail(t, 0):
                 c.start()
         xn_in(0).start()
-        for c in h_in(0):
-            c.start()
-        w2_c(0).wait_recv()
         rem, zero = jnp.int32(REM), jnp.int32(0)
-        w2_in(rem, zero, 1, True)
-        arrive(0)
-        w2_in(rem, zero, 1, False)
+
+        def rest():
+            for c in h_in(0):
+                c.start()
+            w2_c(0).wait_recv()
+            w2_in(rem, zero, 1, True)
+
+        arrive(0, rest)
 
         def tile_(i, carry):
             xn_in(i).wait()
@@ -680,6 +715,7 @@
                         pltpu.make_async_copy(act.at[0, :, at : at + w], h_at(i, q, t0 + off, w), h_sem.at[t, q])
                     )
                     out[-1].start()
+            pl.when(i == 0)(lambda: w2_in(rem, zero, 1, False))
             off, w = tail[final]
             n = fr - w
             slot = _where(i == 0, 0, 1)
@@ -739,16 +775,19 @@
         pl.when(early)(junction)
         second_product(_where(early, 0, BREAK2), _where(early, BREAK2, len(VISITS)))
 
-    @pl.loop(0, N1 + 1)
+    p_x(2, LAST).wait_recv()
+
+    @pl.loop(0, N1)
     def _(j):
-        w1_cr(j).wait_send()
-
-    @pl.loop(0, N1 + 1)
+        w1_c(j).wait_send()
+
+    @pl.loop(0, NT)
     def _(j):
-        @pl.when(j != NR - 1)
-        def _():
-            w1_yr(j).wait_send()
-            w1_f(j).wait_send()
+        w1_y(j).wait_send()
+        w1_f(j).wait_send()
+
+    for c in (w1_yo(), w1_ye(), w1_fo(), w1_fe(), w1_ce()):
+        c.wait_send()
 
     for t in range(len(tail)):
         w1_yt(t).wait_send()
@@ -804,6 +843,7 @@
         half, fq = w1.shape
         sub = rows // 4
         c1, c2 = fq // N1, half // N2
+        ce = fq - NT * c1 - sum(w for _, w in _tail(c1))
 
         def hbm(*shape, dtype=BF16):
             return jax.ShapeDtypeStruct(shape, dtype)
@@ -812,11 +852,11 @@
         outs = (
             hbm(rows, d),
             hbm(sub, c2, dtype=F32),
-            hbm(sub, c2, dtype=F32),
+            hbm(2 * sub, c2, dtype=F32),
             hbm(2 * rows, d),
-            hbm(half, c1), hbm(half, fq + c1), hbm(half, fq + c1), hbm(half, fq + c1),
-            hbm(c1, half), hbm(fq + c1, half), hbm(fq + c1, half), hbm(fq + c1, half),
-            hbm(2 * rows, 2 * (fq + c1)),
+            hbm(half, 2 * c1), *[hbm(half, fq + 2 * c1) for _ in range(3)],
+            hbm(ce, half), *[hbm(fq + ce, half) for _ in range(3)],
+            hbm(2 * rows, 2 * (fq + ce)),
             hbm(rows, d, dtype=F32), hbm(rows, d, dtype=F32), hbm(rows, d, dtype=F32),
         )
         sent = (NX, 2, N1 + 3, N1 + 1, N1 + 3, 3 * N2, N2 + 1, 2 * N2, 8 * N2)
@@ -836,7 +876,7 @@
                 pltpu.VMEM((2, sub, c2), BF16),
                 pltpu.VMEM((sub, c2), BF16),
                 pltpu.VMEM((1, d), F32),
-                *(dma(n) for n in ((2, 2), (2, 4), (3, 2), (3,), (3,), (2, 3), (2, 2, 2))),
+                *(dma(n) for n in ((2, 2), (2, 4), (4, 2), (3,), (3,), (2, 3), (2, 2, 2))),
                 *(dma((n,)) for n in sent for _ in BOTH),
             ],
             compiler_params=pltpu.CompilerParams(
@@ -854,9 +894,13 @@
             compiler_params=pltpu.CompilerParams(vmem_limit_bytes=40_000_000),
             cost_estimate=pl.CostEstimate(flops=30_000_000_000, bytes_accessed=4 * rows * d, transcendentals=0),
         )(out[0])
-        at = (3 * sub, (1 - lax.axis_index("fsdp")) * half + (N2 - 1) * c2)
-        tile = lax.dynamic_slice(x, at, (sub, c2)).astype(F32) + (out[2] + got)
-        return lax.dynamic_update_slice(y, tile.astype(BF16), at)
+        col = (1 - lax.axis_index("fsdp")) * half + (N2 - 1) * c2
+        recv = (out[-1][2 * sub : 3 * sub, LAST * c2 :], got)
+        for i in BOTH:
+            at = ((2 + i) * sub, col)
+            total = out[2][i * sub : (i + 1) * sub] + recv[i]
+            y = lax.dynamic_update_slice(y, (lax.dynamic_slice(x, at, (sub, c2)).astype(F32) + total).astype(BF16), at)
+        return y
 
     return jax.shard_map(
         body,

time: 1850 us -> 1850 us (level)
  no operation moved by 1% of the time
where the time goes in v7:
time: 1850 us
  Pallas kernels  1840 us (99%)
    pallas_call x1, Pallas kernels, body(): pl.pallas_call(_kernel, name='mlp', out_shape=outs, in_specs=[pl.BlockSpe...  1830 us
  transfers between devices with their start and end apart: 1, of which 1 were waited for; matrix products, arithmetic and copies ran while one was open for 0% of the time, Pallas kernels for 1%

profile of v7, /device:TPU:0, one launch (start us, length us, event | category | flops | bytes accessed | tf_op | source)
XLA Modules:
  0.0 1852.3 jit_solution(13465388497008656960)
XLA Ops:
  0.0 1827.6 %mlp.1 = (bf16[2048,6144]{1,0:T(8,128)(2,1)}, f32[512,512]{1,0:T(8,128)}, f32[1024,512]{1,0:T(8,128)}, bf16[4096,6144]{1,0:T(8,128)(2,1)}, bf16[3072,1024]{1,0:T...) custom-call(bf16[2048,6144]{1,0:T(8,128)(2,1)} %x.1, ...), custom_call_target="tpu_custom_call" | custom-call | tf_op jit(solution)/shard_map/mlp/pallas_call | solution.py:863
  1827.6 1.5 collective-permute-start
  1829.1 0.0 copy-start
  1829.1 17.4 put.1
  1846.5 0.0 copy-done
  1846.5 2.5 fusion
  1849.0 1.2 collective-permute-done
  1850.2 2.1 fusion.1
Async XLA Ops:
  1827.6 22.6 %collective-permute-start = (f32[512,512]{1,0:T(8,128)}, f32[512,512]{1,0:T(8,128)S(1)}, u32[]{:S(2)}, u32[]{:S(2)}) collective-permute-start(f32[512,512]{1,0:T(8,128)} %get-tuple-element.12), channel_id=1, source_target_pairs={{0,2},{1,3},{2,0},{3,1},{4,6},{5,7},{6,4},{7,5}} | collective-permute-start | bytes 3145736 | tf_op jit(solution)/shard_map/ppermute | solution.py:886
  1829.1 17.4 copy-start

commit v8 on v7

--- a/solution.py
+++ b/solution.py
@@ -39,14 +39,13 @@
 VISITS = (
     *map(R, range(1, 6)),
     A(0), A(1), R(6), A(2), B(0), B(1), A(3), R(7), B(2), A(4), A(5), R(8), B(3), A(6), A(7), B(4), B(5),
-    R(9), A(8), B(6), A(9), B(7), R(10), B(8), A(10), R(11), A(11), B(9), B(10), B(11),
+    R(9), A(8), A(9), R(10), A(10), R(11), A(11), *map(B, range(N2, N2 + N2)),
 )
 BREAK2 = 4
-PASS_F = {A(1): 0, B(1): 1, A(5): 2, B(5): 3, B(7): 4, R(11): 5}
-PASS_G = {B(4): 0, A(11): 1, B(9): 2, B(10): 3}
+PASS_F = {A(1): 0, B(1): 1, A(5): 2, B(5): 3, A(9): 4, R(11): 5}
+PASS_G = {A(11): 0, B(6): 1, B(7): 2, B(9): 3, B(10): 4, B(11): 5}
 SEND_F = {R(2): (2,), R(5): (3, 4), R(7): (5,)}
-SEND_G = {R(2): (0,), R(7): (1, 2, 3)}
-PARTS_G = ((0, 3), (3, 1), (4, 1), (5, 1))
+SEND_G = {R(7): range(N2)}
 
 
 def _tail(c1):
@@ -178,15 +177,11 @@
         at = (pl.ds(0, fr), cols2(k))
         return remote(w2.at[at], w2far.at[at], w2y_s.at[k], w2y_r.at[k], to_y)
 
-    def cols_g(g):
-        k, n = PARTS_G[g]
-        return pl.ds(k * c2, n * c2)
-
     def w2_yg(g):
-        at, to, n = (pl.ds(fr, ce), cols_g(g)), (pl.ds(fq, ce), cols_g(g)), N2 + g + g
+        at, to, n = (pl.ds(fr, ce), cols2(g)), (pl.ds(fq, ce), cols2(g)), N2 + g + g
         return (
             remote(w2.at[at], w2far.at[at], w2y_s.at[n], w2y_r.at[n], to_y),
-            remote(w2e.at[:, cols_g(g)], w2far.at[to], w2y_s.at[n + 1], w2y_r.at[n + 1], to_y),
+            remote(w2e.at[:, cols2(g)], w2far.at[to], w2y_s.at[n + 1], w2y_r.at[n + 1], to_y),
         )
 
     def w2_c(k):
@@ -201,7 +196,7 @@
         return remote(w2far.at[at], w2sf.at[at], w2f_s.at[k], w2f_r.at[k], to_c)
 
     def w2_fg(g):
-        at = (pl.ds(fr, 2 * ce), cols_g(g))
+        at = (pl.ds(fr, 2 * ce), cols2(g))
         return remote(w2far.at[at], w2sf.at[at], w2f_s.at[N2 + g], w2f_r.at[N2 + g], to_c)
 
     def xrows(t):
@@ -465,7 +460,7 @@
             wait_or_start(pltpu.make_async_copy(x.at[hrows(i), pl.ds(ycol, c2)], xin.at[slot], in_sem.at[slot, 1]))
             if go:
 
-                @pl.when(k < LAST)
+                @pl.when((k < LAST) | (i < 2))
                 def _():
                     p_x(i, k).wait_recv()
                     p_in(i, k, slot).start()
@@ -516,9 +511,8 @@
                 todo.append(lambda k=k: w2_c(k).wait_recv() if k < N2 else w2_ff(k - N2).wait_recv())
             if n == min(at[B(k)] for k in range(N2)):
                 todo.append(lambda: w2_ce().wait_recv())
-            for g, (k0, nk) in enumerate(PARTS_G):
-                if n == min(at[B(N2 + k)] for k in range(k0, k0 + nk)):
-                    todo.append(lambda g=g: w2_fg(g).wait_recv())
+            if visit[0] == END and visit[1] >= N2:
+                todo.append(lambda g=visit[1] - N2: w2_fg(g).wait_recv())
             if todo:
 
                 @pl.when(v == n)
@@ -568,14 +562,14 @@
                 slot = i % 2
                 last = i == 3
 
+                @pl.when(more | (i < 3))
+                def _():
+                    a2_in(_where(last, ntyp, typ), _where(last, nk, k), _where(last, 0, i + 1), 1 - slot, True)
+
                 @pl.when(last & more)
                 def _():
                     arrive2(v + 1)
                     w2_in(ntyp, nk, 1 - wslot, True)
-
-                @pl.when(more | (i < 3))
-                def _():
-                    a2_in(_where(last, ntyp, typ), _where(last, nk, k), _where(last, 0, i + 1), 1 - slot, True)
 
                 a2_in(typ, k, i, slot, False)
                 pl.when(i == 0)(lambda: w2_in(typ, k, wslot, False))
@@ -603,11 +597,6 @@
 
                 @pl.when((typ == END) & inside)
                 def _():
-                    @pl.when(k == LAST)
-                    def _():
-                        p_x(i, k).wait_recv()
-                        p_in(i, k, slot).start()
-
                     p_in(i, k, slot).wait()
                     total = (pback[slot] + pout[slot]) + pin[slot]
                     yout[...] = (xin[slot].astype(F32) + total).astype(BF16)
@@ -802,7 +791,7 @@
     w1_e().wait_send()
     w2_e().wait_send()
     w2_ce().wait_send()
-    for g in range(len(PARTS_G)):
+    for g in range(N2):
         for c in w2_yg(g):
             c.wait_send()
         w2_fg(g).wait_send()

time: 1850 us -> 1840 us (level)
  no operation moved by 1% of the time
where the time goes in v8:
time: 1840 us
  Pallas kernels  1830 us (99%)
    pallas_call x1, Pallas kernels, body(): pl.pallas_call(_kernel, name='mlp', out_shape=outs, in_specs=[pl.BlockSpe...  1810 us
  transfers between devices with their start and end apart: 1, of which 1 were waited for; matrix products, arithmetic and copies ran while one was open for 0% of the time, Pallas kernels for 1%

profile of v8, /device:TPU:0, one launch (start us, length us, event | category | flops | bytes accessed | tf_op | source)
XLA Modules:
  0.0 1841.1 jit_solution(182347995822151865)
XLA Ops:
  0.0 1814.9 %mlp.1 = (bf16[2048,6144]{1,0:T(8,128)(2,1)}, f32[512,512]{1,0:T(8,128)}, f32[1024,512]{1,0:T(8,128)}, bf16[4096,6144]{1,0:T(8,128)(2,1)}, bf16[3072,1024]{1,0:T...) custom-call(bf16[2048,6144]{1,0:T(8,128)(2,1)} %x.1, ...), custom_call_target="tpu_custom_call" | custom-call | tf_op jit(solution)/shard_map/mlp/pallas_call | solution.py:852
  1814.9 1.5 collective-permute-start
  1816.4 0.0 copy-start
  1816.4 17.4 put.1
  1833.9 0.0 copy-done
  1833.9 2.5 fusion
  1836.3 2.6 collective-permute-done
  1839.0 2.1 fusion.1
Async XLA Ops:
  1814.9 24.0 %collective-permute-start = (f32[512,512]{1,0:T(8,128)}, f32[512,512]{1,0:T(8,128)S(1)}, u32[]{:S(2)}, u32[]{:S(2)}) collective-permute-start(f32[512,512]{1,0:T(8,128)} %get-tuple-element.12), channel_id=1, source_target_pairs={{0,2},{1,3},{2,0},{3,1},{4,6},{5,7},{6,4},{7,5}} | collective-permute-start | bytes 3145736 | tf_op jit(solution)/shard_map/ppermute | solution.py:875
  1816.4 17.4 copy-start

commit v9 on v8

--- a/solution.py
+++ b/solution.py
@@ -196,8 +196,11 @@
         return remote(w2far.at[at], w2sf.at[at], w2f_s.at[k], w2f_r.at[k], to_c)
 
     def w2_fg(g):
-        at = (pl.ds(fr, 2 * ce), cols2(g))
-        return remote(w2far.at[at], w2sf.at[at], w2f_s.at[N2 + g], w2f_r.at[N2 + g], to_c)
+        out = []
+        for part, row in enumerate((fr, fq)):
+            at, n = (pl.ds(row, ce), cols2(g)), N2 + g + g + part
+            out.append(remote(w2far.at[at], w2sf.at[at], w2f_s.at[n], w2f_r.at[n], to_c))
+        return out
 
     def xrows(t):
         return pl.ds(pl.multiple_of(t * piece, piece), piece)
@@ -327,6 +330,8 @@
             pl.when(j == NT)(lambda: w1_fo().wait_recv())
             pl.when(j == NR)(lambda: w1_c(j).wait_recv())
             pl.when(j == N1)(lambda: (w1_ce().wait_recv(), w1_fe().wait_recv()) and None)
+
+        pl.when((j == NT - 1) & (q == 1) & (m == 3))(lambda: (w1_yt(0).wait_recv(), w1_ft(0).start()) and None)
 
         @pl.when(first & (q == 0))
         def _():
@@ -477,8 +482,13 @@
             load(1, fr, fr, sib, 0, kk)
 
         def rest(own, ext, ext_at, sib, kk):
-            for n, (ref, from_) in enumerate(((own, fr), (sib, fr), (ext, ext_at), (sib, fq))):
-                load(n, n * ce, ce, ref, from_, kk)
+            load(0, 0, ce, own, fr, kk)
+            load(2, 2 * ce, ce, ext, ext_at, kk)
+            if go and sib is w2sf:
+                for c in w2_fg(kk):
+                    c.wait_recv()
+            load(1, ce, ce, sib, fr, kk)
+            load(3, 3 * ce, ce, sib, fq, kk)
 
         def both(side, kk, own, ext, ext_at, sib):
             pl.when(side & (typ != END))(lambda: main(own, sib, kk))
@@ -505,14 +515,12 @@
                 todo.append(lambda u=u: (w2_yf(u).wait_recv(), w2_ff(u).start()))
             if visit in PASS_G:
                 g = PASS_G[visit]
-                todo.append(lambda g=g: ([c.wait_recv() for c in w2_yg(g)], w2_fg(g).start()))
+                todo.append(lambda g=g: [(c.wait_recv(), f.start()) for c, f in zip(w2_yg(g), w2_fg(g))])
             if visit[0] == REM:
                 k = visit[1]
                 todo.append(lambda k=k: w2_c(k).wait_recv() if k < N2 else w2_ff(k - N2).wait_recv())
             if n == min(at[B(k)] for k in range(N2)):
                 todo.append(lambda: w2_ce().wait_recv())
-            if visit[0] == END and visit[1] >= N2:
-                todo.append(lambda g=visit[1] - N2: w2_fg(g).wait_recv())
             if todo:
 
                 @pl.when(v == n)
@@ -650,11 +658,11 @@
             u = jnp.dot(act[1, block, :d], wb[0, r : r + d, at : at + 2 * tail[t][1]], preferred_element_type=F32)
             return jax.nn.gelu(u, approximate=True).astype(BF16)
 
-        def arrive(t, meanwhile=lambda: None):
-            w1_yt(t).wait_recv()
-            w1_ft(t).start()
+        def reach(t):
+            if t == final:
+                w1_yt(t).wait_recv()
+                w1_ft(t).start()
             w_tail(t, 1)[0].start()
-            meanwhile()
             if t == final:
                 w1_yo().start()
                 w1_e().wait_recv()
@@ -662,6 +670,8 @@
                 w2_yf(0).start()
                 w2_yf(1).start()
                 w2_e().wait_recv()
+
+        def arrive(t):
             w1_ft(t).wait_recv()
             w_tail(t, 1)[1].start()
             if t == final:
@@ -684,7 +694,9 @@
             w2_c(0).wait_recv()
             w2_in(rem, zero, 1, True)
 
-        arrive(0, rest)
+        reach(0)
+        rest()
+        arrive(0)
 
         def tile_(i, carry):
             xn_in(i).wait()
@@ -704,7 +716,12 @@
                         pltpu.make_async_copy(act.at[0, :, at : at + w], h_at(i, q, t0 + off, w), h_sem.at[t, q])
                     )
                     out[-1].start()
-            pl.when(i == 0)(lambda: w2_in(rem, zero, 1, False))
+
+            @pl.when(i == 0)
+            def _():
+                reach(final)
+                w2_in(rem, zero, 1, False)
+
             off, w = tail[final]
             n = fr - w
             slot = _where(i == 0, 0, 1)
@@ -794,7 +811,8 @@
     for g in range(N2):
         for c in w2_yg(g):
             c.wait_send()
-        w2_fg(g).wait_send()
+        for c in w2_fg(g):
+            c.wait_send()
 
     @pl.loop(0, NX)
     def _(t):
@@ -848,7 +866,7 @@
             hbm(2 * rows, 2 * (fq + ce)),
             hbm(rows, d, dtype=F32), hbm(rows, d, dtype=F32), hbm(rows, d, dtype=F32),
         )
-        sent = (NX, 2, N1 + 3, N1 + 1, N1 + 3, 3 * N2, N2 + 1, 2 * N2, 8 * N2)
+        sent = (NX, 2, N1 + 3, N1 + 1, N1 + 3, 3 * N2, N2 + 1, 3 * N2, 8 * N2)
         out = pl.pallas_call(
             _kernel,
             name="mlp",

time: 1840 us -> 1850 us (level)
  no operation moved by 1% of the time
where the time goes in v9:
time: 1850 us
  Pallas kernels  1840 us (99%)
    pallas_call x1, Pallas kernels, body(): pl.pallas_call(_kernel, name='mlp', out_shape=outs, in_specs=[pl.BlockSpe...  1820 us
  transfers between devices with their start and end apart: 1, of which 1 were waited for; matrix products, arithmetic and copies ran while one was open for 0% of the time, Pallas kernels for 1%

profile of v9, /device:TPU:0, one launch (start us, length us, event | category | flops | bytes accessed | tf_op | source)
XLA Modules:
  0.0 1847.7 jit_solution(9372386144734679590)
XLA Ops:
  0.0 1820.6 %mlp.1 = (bf16[2048,6144]{1,0:T(8,128)(2,1)}, f32[512,512]{1,0:T(8,128)}, f32[1024,512]{1,0:T(8,128)}, bf16[4096,6144]{1,0:T(8,128)(2,1)}, bf16[3072,1024]{1,0:T...) custom-call(bf16[2048,6144]{1,0:T(8,128)(2,1)} %x.1, ...), custom_call_target="tpu_custom_call" | custom-call | tf_op jit(solution)/shard_map/mlp/pallas_call | solution.py:870
  1820.6 1.5 collective-permute-start
  1822.1 0.0 copy-start
  1822.1 17.4 put.1
  1839.5 0.0 copy-done
  1839.5 2.5 fusion
  1842.0 3.6 collective-permute-done
  1845.6 2.1 fusion.1
Async XLA Ops:
  1820.6 25.0 %collective-permute-start = (f32[512,512]{1,0:T(8,128)}, f32[512,512]{1,0:T(8,128)S(1)}, u32[]{:S(2)}, u32[]{:S(2)}) collective-permute-start(f32[512,512]{1,0:T(8,128)} %get-tuple-element.12), channel_id=1, source_target_pairs={{0,2},{1,3},{2,0},{3,1},{4,6},{5,7},{6,4},{7,5}} | collective-permute-start | bytes 3145736 | tf_op jit(solution)/shard_map/ppermute | solution.py:893
  1822.1 17.4 copy-start
